TPU v7x, 256 devices: a whole 4x4x8 slice. The times are simulated.
256 devices in a mesh: gx: 8 (over z_lo, core), gy: 32 (over y, x, z_hi).
Axes of the slice: x: 4, y: 4, z: 8 (z_hi: 2, z_lo: 4; z = z_hi * 4 + z_lo), core: 2. Of those that a mesh axis runs over, the one named last changes fastest.
Arguments:
- data: float32 [128, 512, 128], P('gx', 'gy'), may hold values from -6 to 6
- precond: float32 [128, 512, 128], P('gx', 'gy'), may hold values from 0.5 to 2
- psf: float32 [8, 32, 17, 17, 17], P('gx', 'gy'), may hold values from -0.05 to 0.05
Outputs:
- model: float32 [128, 512, 128], P('gx', 'gy')
- residual: float32 [128, 512, 128], P('gx', 'gy')
All inputs are finite; a program needn't handle non-finite values.
Results may differ from a plain program's by a relative error of at most 0.0003.
Values sent between devices are 32-bit elements; how exact they have to be, the bound alone decides.
No kernel may reach another device: no remote copies, remote signals or barrier semaphores. Data moves between devices by JAX's collectives and lax.ppermute only.
A program may use at most 64 MiB of HBM per device.

v0:
```python
import jax
import jax.numpy as jnp
from jax import lax
from jax.experimental import pallas as pl
from jax.experimental.pallas import tpu as pltpu
from jax.sharding import PartitionSpec as P

ITERS = 2
relaxation = 0.7

H = 8
TAPS = 17
T = 16
Z = 128
GROUP = 32
SPAN = 640
ROWS = 2 * TAPS * 8 * T
PACKED = 88
VMEM = pl.BlockSpec(memory_space=pltpu.VMEM)


def call(kernel, outs, scratch=(), limit=None):
    return pl.pallas_call(
        kernel,
        out_shape=outs,
        scratch_shapes=list(scratch),
        compiler_params=pltpu.CompilerParams(vmem_limit_bytes=limit),
    )


def f32(*shape):
    return jax.ShapeDtypeStruct(shape, jnp.float32)


def prepare(d_ref, p_ref, psf_ref, v_ref, up_ref, down_ref, t_ref):
    v = d_ref[...] * p_ref[...]
    v_ref[...] = v
    up_ref[...] = v[:, H:, :]
    down_ref[: T * H, :] = v[:, :H, :].reshape(T * H, Z)
    t_ref[...] = jnp.zeros_like(t_ref)
    for a in range(TAPS):
        t_ref[GROUP * a : GROUP * a + TAPS, :TAPS] = psf_ref[0, 0, a]
    turned = t_ref[...].T
    for u in range(5):
        down_ref[T * H + u * TAPS : T * H + (u + 1) * TAPS, :] = turned[:TAPS, u * 128 : (u + 1) * 128]
    down_ref[T * H + 5 * TAPS :, :] = jnp.zeros((PACKED - 5 * TAPS, Z), jnp.float32)


def pack_first(v_ref, before_ref, down_ref, after_ref, wide_ref, up_ref, low_ref):
    wide_ref[:, :H, :] = before_ref[...]
    wide_ref[:, H : H + T, :] = v_ref[...]
    wide_ref[:, H + T :, :] = after_ref[: T * H, :].reshape(T, H, Z)
    up_ref[...] = wide_ref[H:]
    low_ref[: H * GROUP, :] = wide_ref[:H].reshape(H * GROUP, Z)
    low_ref[H * GROUP : H * GROUP + PACKED, :] = down_ref[T * H :, :]
    low_ref[H * GROUP + PACKED :, :] = after_ref[T * H :, :]


def pack_next(v_ref, before_ref, after_ref, wide_ref, up_ref, low_ref):
    wide_ref[:, :H, :] = before_ref[...]
    wide_ref[:, H : H + T, :] = v_ref[...]
    wide_ref[:, H + T :, :] = after_ref[...]
    up_ref[...] = wide_ref[H:]
    low_ref[...] = wide_ref[:H]


def halves(v):
    high = v.astype(jnp.bfloat16)
    low = (v - high.astype(jnp.float32)).astype(jnp.bfloat16)
    return jnp.concatenate([high, low], axis=1)


def stationary(v):
    both = halves(v)
    return jnp.concatenate([both, both], axis=0)


def slot(term, m, r, u):
    return ((term * 2 + m) * 4 + r) * 5 + u


def build(own_ref, nextx_ref, nexty_ref, corner_ref, wa_ref, wb_ref, rows_ref, last_x, last_y):
    def spread(ref):
        full = [ref[u * TAPS : (u + 1) * TAPS, :] for u in range(5)]
        return jnp.concatenate(full, axis=1)

    own = spread(own_ref)
    nextx = jnp.where(last_x, own, spread(nextx_ref))
    nexty = jnp.where(last_y, own, spread(nexty_ref))
    corner = jnp.where(last_y, nextx, jnp.where(last_x, nexty, spread(corner_ref)))
    for m, (near, far) in enumerate(((own, nexty), (nextx, corner))):
        for term, table in enumerate((near, far - near)):
            for r in range(4):
                rolled = table if r == 0 else pltpu.roll(table, GROUP * r, 1)
                for u in range(5):
                    rows_ref[slot(term, m, r, u), :TAPS, :] = rolled[:, u * 128 : (u + 1) * 128]
    along = lax.broadcasted_iota(jnp.int32, (H, Z), 0).astype(jnp.float32)
    steps = [(along + (0.5 + H * half)) / T for half in range(2)]
    zero = jnp.zeros((T, 128), jnp.bfloat16)

    @pl.loop(0, TAPS)
    def _(c):
        def base(x):
            return pl.multiple_of((((x // 8) * TAPS + c) * 8 + x % 8) * T, T)

        for r in range(4):
            for u in range(5):
                node = []
                for m in range(2):
                    near = rows_ref[slot(0, m, r, u), pl.ds(c, H, stride=0), :]
                    step = rows_ref[slot(1, m, r, u), pl.ds(c, H, stride=0), :]
                    node.append(
                        jnp.concatenate(
                            [
                                pltpu.roll(near + steps[half] * step, H * half, 1, stride=1, stride_axis=0)
                                for half in range(2)
                            ],
                            axis=0,
                        )
                    )
                across = node[1] - node[0]
                for q in range(4):
                    x = 4 * q + r
                    w = node[0] + ((x + 0.5) / T) * across
                    high = w.astype(jnp.bfloat16)
                    low = (w - high.astype(jnp.float32)).astype(jnp.bfloat16)
                    tile = q + u
                    if 2 <= tile < 6:
                        wa_ref[pl.ds(base(x), T), (tile - 2) * 128 : (tile - 1) * 128] = high
                        wa_ref[pl.ds(base(x), T), 512 + (tile - 2) * 128 : 512 + (tile - 1) * 128] = low
                    else:
                        at = (tile % 2) * 128
                        wb_ref[pl.ds(base(x), T), at : at + 128] = high
                        wb_ref[pl.ds(base(x), T), 256 + at : 256 + at + 128] = low
            for q, ref, at, width in ((0, wa_ref, 384, 512), (1, wb_ref, 0, 256), (2, wb_ref, 128, 256), (3, wa_ref, 0, 512)):
                ref[pl.ds(base(4 * q + r), T), at : at + 128] = zero
                ref[pl.ds(base(4 * q + r), T), width + at : width + at + 128] = zero


def product(w, v):
    both = jnp.dot(w, v, preferred_element_type=jnp.float32)
    return both[:, :Z] + both[:, Z:]


def inner_part(wide_ref, wa_ref, r_ref):
    v = stationary(wide_ref[...].reshape(T * GROUP, Z))
    for h in range(2):
        rows = slice(h * TAPS * 128, (h + 1) * TAPS * 128)
        r_ref[rows, :] = product(wa_ref[rows, :], v)


def outer_part(before_ref, after_ref, wb_ref, r_ref, out_ref):
    lane = lax.broadcasted_iota(jnp.int32, (128, Z), 1)
    for h, side in enumerate((before_ref, after_ref)):
        v = stationary(side[...])
        total = None
        for c in range(TAPS):
            at = slice((h * TAPS + c) * 128, (h * TAPS + c + 1) * 128)
            part = r_ref[at, :] + product(wb_ref[at, :], v)
            if c != H:
                part = pltpu.roll(part, (H - c) % Z, 1)
                part = jnp.where((lane >= H - c) & (lane < Z + H - c), part, 0.0)
            total = part if total is None else total + part
        out_ref[h * 8 : (h + 1) * 8] = total.reshape(8, T, Z)


def step_one(d_ref, p_ref, wide_ref, before_ref, low_ref, down_ref, nexty_ref, flag_ref,
             wa_ref, wb_ref, model_ref, rows_ref, r_ref, k_ref):
    last_x = flag_ref[0] == 1
    last_y = flag_ref[1] == 1
    side = H * GROUP
    build(
        down_ref.at[T * H :, :],
        low_ref.at[side : side + PACKED, :],
        nexty_ref.at[T * H :, :],
        low_ref.at[side + PACKED :, :],
        wa_ref, wb_ref, rows_ref, last_x, last_y,
    )
    inner_part(wide_ref, wa_ref, r_ref)
    outer_part(before_ref, low_ref.at[:side, :], wb_ref, r_ref, k_ref)
    v = wide_ref[:, H : H + T, :]
    residual = d_ref[...] - (v + k_ref[...])
    model_ref[...] = v + relaxation * p_ref[...] * residual


def step_two_inner(wide_ref, wa_ref, r_ref):
    inner_part(wide_ref, wa_ref, r_ref)


def step_two_outer(d_ref, p_ref, v_ref, before_ref, after_ref, wb_ref, r_ref, model_ref, residual_ref, k_ref):
    outer_part(before_ref, after_ref, wb_ref, r_ref, k_ref)
    v = v_ref[...]
    residual = d_ref[...] - (v + k_ref[...])
    residual_ref[...] = residual
    model_ref[...] = v + relaxation * p_ref[...] * residual


def passed_along(shard, axis, by):
    length = lax.axis_size(axis)
    return lax.ppermute(shard, axis, [(i, i + by) for i in range(length) if 0 <= i + by < length])


def pinned(shape, dtype):
    return pltpu.VMEM(shape, dtype)


def local(data, precond, psf):
    flags = jnp.stack([lax.axis_index("gx") == lax.axis_size("gx") - 1, lax.axis_index("gy") == lax.axis_size("gy") - 1]).astype(jnp.int32)
    v, up, down = call(
        prepare, (f32(T, T, Z), f32(T, H, Z), f32(T * H + PACKED, Z)), [pltpu.VMEM((SPAN, 128), jnp.float32)]
    )(data, precond, psf)
    before = passed_along(up, "gy", 1)
    after = passed_along(down, "gy", -1)
    wide, up, low = call(pack_first, (f32(T, GROUP, Z), f32(H, GROUP, Z), f32(H * GROUP + 2 * PACKED, Z)))(v, before, down, after)
    above = passed_along(up, "gx", 1)
    below = passed_along(low, "gx", -1)
    smem = pl.BlockSpec(memory_space=pltpu.SMEM)
    wa, wb, v = pl.pallas_call(
        step_one,
        out_shape=(
            pinned((ROWS, 1024), jnp.bfloat16),
            pinned((ROWS, 512), jnp.bfloat16),
            f32(T, T, Z),
        ),
        in_specs=[VMEM] * 7 + [smem],
        out_specs=(VMEM, VMEM, VMEM),
        scratch_shapes=[
            pltpu.VMEM((80, 24, 128), jnp.float32),
            pltpu.VMEM((ROWS, Z), jnp.float32),
            pltpu.VMEM((T, T, Z), jnp.float32),
        ],
        compiler_params=pltpu.CompilerParams(vmem_limit_bytes=40 << 20),
    )(data, precond, wide, above.reshape(H * GROUP, Z), below, down, after, flags)
    before = passed_along(v[:, H:, :], "gy", 1)
    after = passed_along(v[:, :H, :], "gy", -1)
    wide, up, low = call(pack_next, (f32(T, GROUP, Z), f32(H, GROUP, Z), f32(H, GROUP, Z)))(v, before, after)
    above = passed_along(up, "gx", 1)
    below = passed_along(low, "gx", -1)
    part = pl.pallas_call(
        step_two_inner,
        out_shape=pinned((ROWS, Z), jnp.float32),
        in_specs=[VMEM, VMEM],
        out_specs=VMEM,
        compiler_params=pltpu.CompilerParams(vmem_limit_bytes=24 << 20),
    )(wide, wa)
    return pl.pallas_call(
        step_two_outer,
        out_shape=(f32(T, T, Z), f32(T, T, Z)),
        in_specs=[VMEM] * 7,
        out_specs=(VMEM, VMEM),
        scratch_shapes=[pltpu.VMEM((T, T, Z), jnp.float32)],
        compiler_params=pltpu.CompilerParams(vmem_limit_bytes=16 << 20),
    )(data, precond, v, above.reshape(H * GROUP, Z), below.reshape(H * GROUP, Z), wb, part)


def solution(mesh):
    placed = (P("gx", "gy", None), P("gx", "gy", None), P("gx", "gy", None, None, None))
    return jax.shard_map(
        local,
        mesh=mesh,
        in_specs=placed,
        out_specs=(P("gx", "gy", None), P("gx", "gy", None)),
        check_vma=False,
    )
```

profile of v0, /device:TPU:57, one launch (start us, length us, event | category | flops | bytes accessed | tf_op | source)
XLA Modules:
  0.0 91.0 jit_solution(12257876342831200122)
XLA Ops:
  0.6 1.6 %copy.5.psf_ref = f32[1,1,17,17,17]{4,3,2,1,0:T(8,128)} copy(f32[1,1,17,17,17]{4,1,3,2,0:T(1,128)} %param.5) | data formatting | bytes 39304 | tf_op args[2]
  2.2 1.9 %shard_map.50 = (f32[16,16,128]{2,1,0:T(8,128)}, f32[16,8,128]{2,1,0:T(8,128)}, f32[216,128]{1,0:T(8,128)}) custom-call(f32[16,16,128]{2,1,0:T(8,128)} %d_ref.5, f32[16,16,128]{2,1,0:T(8,128)} %p_ref.5, f32[1,1,17,17,17]{4,3,2,1,0:T(8,128)} %copy.5.psf_ref), custom_call_target="tpu_custom_call" | custom-call | tf_op jit(solution)/shard_map/pallas_call | solution.py:209
  4.1 10.3 %collective-permute-start.1 = (f32[216,128]{1,0:T(8,128)}, f32[216,128]{1,0:T(8,128)S(1)}, u32[]{:S(2)}, u32[]{:S(2)}) collective-permute-start(f32[216,128]{1,0:T(8,128)} %get-tuple-element.16.down_ref), channel_id=1, source_target_pairs={{1,0},{2,1},{3,2},{4,3},{5,4},{6,5},{7,6},{8,7},{9,8},{10,9},{11,1... | collective-permute-start | bytes 331784 | tf_op jit(solution)/shard_map/ppermute | solution.py:200
  14.4 1.9 %collective-permute-start = (f32[16,8,128]{2,1,0:T(8,128)}, f32[16,8,128]{2,1,0:T(8,128)S(1)}, u32[]{:S(2)}, u32[]{:S(2)}) collective-permute-start(f32[16,8,128]{2,1,0:T(8,128)} %get-tuple-element.15), channel_id=1, source_target_pairs={{0,1},{1,2},{2,3},{3,4},{4,5},{5,6},{6,7},{7,8},{8,9},{9,10},{10,1... | collective-permute-start | bytes 196616 | tf_op jit(solution)/shard_map/ppermute | solution.py:200
  16.3 10.2 %collective-permute-done.before_ref = f32[16,8,128]{2,1,0:T(8,128)S(1)} collective-permute-done((f32[16,8,128]{2,1,0:T(8,128)}, f32[16,8,128]{2,1,0:T(8,128)S(1)}, u32[]{:S(2)}, u32[]{:S(2)}) %collective-permute-start) | collective-permute-done | bytes 65568 | tf_op jit(solution)/shard_map/ppermute | solution.py:200
  27.2 1.9 %shard_map.51 = (f32[16,32,128]{2,1,0:T(8,128)}, f32[8,32,128]{2,1,0:T(8,128)}, f32[432,128]{1,0:T(8,128)}) custom-call(f32[16,16,128]{2,1,0:T(8,128)} %get-tuple-element.14.v_ref, f32[16,8,128]{2,1,0:T(8,128)} %copy-done.14, f32[216,128]{1,0:T(8,128)} %get-tuple-element.16.down_ref, f32[216,128]{1,0:T(8,128)} %copy-done.10), custom_call_target="tpu_custom_call" | custom-call | tf_op jit(solution)/shard_map/pallas_call | solution.py:214
  29.1 4.0 %collective-permute-start.3 = (f32[432,128]{1,0:T(8,128)}, f32[432,128]{1,0:T(8,128)S(1)}, u32[]{:S(2)}, u32[]{:S(2)}) collective-permute-start(f32[432,128]{1,0:T(8,128)} %get-tuple-element.19), channel_id=1, source_target_pairs={{32,0},{64,32},{96,64},{128,96},{160,128},{192,160},{224,192},{33,... | collective-permute-start | bytes 663560 | tf_op jit(solution)/shard_map/ppermute | solution.py:200
  33.2 2.7 %collective-permute-start.2 = (f32[8,32,128]{2,1,0:T(8,128)}, f32[8,32,128]{2,1,0:T(8,128)S(1)}, u32[]{:S(2)}, u32[]{:S(2)}) collective-permute-start(f32[8,32,128]{2,1,0:T(8,128)} %get-tuple-element.18), channel_id=1, source_target_pairs={{0,32},{32,64},{64,96},{96,128},{128,160},{160,192},{192,224},{1,3... | collective-permute-start | bytes 393224 | tf_op jit(solution)/shard_map/ppermute | solution.py:200
  35.9 2.2 %collective-permute-done.2 = f32[8,32,128]{2,1,0:T(8,128)S(1)} collective-permute-done((f32[8,32,128]{2,1,0:T(8,128)}, f32[8,32,128]{2,1,0:T(8,128)S(1)}, u32[]{:S(2)}, u32[]{:S(2)}) %collective-permute-start.2) | collective-permute-done | bytes 131104 | tf_op jit(solution)/shard_map/ppermute | solution.py:200
  38.1 0.9 copy-done.5
  41.7 0.9 %copy-done.13 = f32[16,32,128]{2,1,0:T(8,128)S(1)} copy-done((f32[16,32,128]{2,1,0:T(8,128)S(1)}, f32[16,32,128]{2,1,0:T(8,128)}, u32[]{:S(2)}) %copy-start.13) | copy-done | bytes 262168
  42.6 8.8 %shard_map.52 = (bf16[4352,1024]{1,0:T(8,128)(2,1)S(1)}, bf16[4352,512]{1,0:T(8,128)(2,1)S(1)}, f32[16,16,128]{2,1,0:T(8,128)S(1)}) custom-call(f32[16,16,128]{2,1,0:T(8,128)S(1)} %copy-done.5, f32[16,16,128]{2,1,0:T(8,128)S(1)} %copy-done.7, f32[16,32,128]{2,1,0:T(8,128)S(1)} %copy-done.13, f32[256,128]{1,0:T(8,128)S(1)} %bitcast.9, ...), custom_call_target="tpu_custom_call" | custom-call | tf_op jit(solution)/shard_map/pallas_call | solution.py:218
  51.5 3.4 %copy-done = bf16[4352,1024]{1,0:T(8,128)(2,1)} copy-done((bf16[4352,1024]{1,0:T(8,128)(2,1)}, bf16[4352,1024]{1,0:T(8,128)(2,1)S(1)}, u32[]{:S(2)}) %copy-start) | copy-done | bytes 8912920
  54.9 2.2 %copy-done.2 = bf16[4352,512]{1,0:T(8,128)(2,1)} copy-done((bf16[4352,512]{1,0:T(8,128)(2,1)}, bf16[4352,512]{1,0:T(8,128)(2,1)S(1)}, u32[]{:S(2)}) %copy-start.2) | copy-done | bytes 4456472
  57.1 2.4 %collective-permute-start.4 = (f32[16,8,128]{2,1,0:T(8,128)S(1)}, f32[16,8,128]{2,1,0:T(8,128)S(1)}, u32[]{:S(2)}, u32[]{:S(2)}) collective-permute-start(f32[16,8,128]{2,1,0:T(8,128)S(1)} %get-tuple-element.27), channel_id=1, source_target_pairs={{0,1},{1,2},{2,3},{3,4},{4,5},{5,6},{6,7},{7,8},{8,9},{9,10},{10,1... | collective-permute-start | bytes 196616 | tf_op jit(solution)/shard_map/ppermute | solution.py:200
  59.5 10.0 %collective-permute-start.5 = (f32[16,8,128]{2,1,0:T(8,128)S(1)}, f32[16,8,128]{2,1,0:T(8,128)S(1)}, u32[]{:S(2)}, u32[]{:S(2)}) collective-permute-start(f32[16,8,128]{2,1,0:T(8,128)S(1)} %get-tuple-element.26), channel_id=1, source_target_pairs={{1,0},{2,1},{3,2},{4,3},{5,4},{6,5},{7,6},{8,7},{9,8},{10,9},{11,1... | collective-permute-start | bytes 196616 | tf_op jit(solution)/shard_map/ppermute | solution.py:200
  69.9 1.5 %collective-permute-done.5.after_ref = f32[16,8,128]{2,1,0:T(8,128)S(1)} collective-permute-done((f32[16,8,128]{2,1,0:T(8,128)S(1)}, f32[16,8,128]{2,1,0:T(8,128)S(1)}, u32[]{:S(2)}, u32[]{:S(2)}) %collective-permute-start.5) | collective-permute-done | bytes 65568 | tf_op jit(solution)/shard_map/ppermute | solution.py:200
  72.0 1.8 %shard_map.53 = (f32[16,32,128]{2,1,0:T(8,128)}, f32[8,32,128]{2,1,0:T(8,128)}, f32[8,32,128]{2,1,0:T(8,128)}) custom-call(f32[16,16,128]{2,1,0:T(8,128)} %copy-done.3, f32[16,8,128]{2,1,0:T(8,128)} %copy-done.15, f32[16,8,128]{2,1,0:T(8,128)} %copy-done.16), custom_call_target="tpu_custom_call" | custom-call | tf_op jit(solution)/shard_map/pallas_call | solution.py:236
  73.7 6.2 %collective-permute-start.6 = (f32[8,32,128]{2,1,0:T(8,128)}, f32[8,32,128]{2,1,0:T(8,128)S(1)}, u32[]{:S(2)}, u32[]{:S(2)}) collective-permute-start(f32[8,32,128]{2,1,0:T(8,128)} %get-tuple-element.21), channel_id=1, source_target_pairs={{0,32},{32,64},{64,96},{96,128},{128,160},{160,192},{192,224},{1,3... | collective-permute-start | bytes 393224 | tf_op jit(solution)/shard_map/ppermute | solution.py:200
  79.9 1.9 %collective-permute-start.7 = (f32[8,32,128]{2,1,0:T(8,128)}, f32[8,32,128]{2,1,0:T(8,128)S(1)}, u32[]{:S(2)}, u32[]{:S(2)}) collective-permute-start(f32[8,32,128]{2,1,0:T(8,128)} %get-tuple-element.22), channel_id=1, source_target_pairs={{32,0},{64,32},{96,64},{128,96},{160,128},{192,160},{224,192},{33,... | collective-permute-start | bytes 393224 | tf_op jit(solution)/shard_map/ppermute | solution.py:200
  81.9 3.5 %copy-done.1 = bf16[4352,1024]{1,0:T(8,128)(2,1)S(1)} copy-done((bf16[4352,1024]{1,0:T(8,128)(2,1)S(1)}, bf16[4352,1024]{1,0:T(8,128)(2,1)}, u32[]{:S(2)}) %copy-start.1) | copy-done | bytes 8912920
  85.4 0.9 %copy-done.12 = f32[16,32,128]{2,1,0:T(8,128)S(1)} copy-done((f32[16,32,128]{2,1,0:T(8,128)S(1)}, f32[16,32,128]{2,1,0:T(8,128)}, u32[]{:S(2)}) %copy-start.12) | copy-done | bytes 262168
  86.3 2.5 %shard_map.54.r_ref = f32[4352,128]{1,0:T(8,128)S(1)} custom-call(f32[16,32,128]{2,1,0:T(8,128)S(1)} %copy-done.12, bf16[4352,1024]{1,0:T(8,128)(2,1)S(1)} %copy-done.1), custom_call_target="tpu_custom_call" | custom-call | tf_op jit(solution)/shard_map/pallas_call | solution.py:239
  88.9 2.1 %shard_map.55 = (f32[16,16,128]{2,1,0:T(8,128)}, f32[16,16,128]{2,1,0:T(8,128)}) custom-call(f32[16,16,128]{2,1,0:T(8,128)S(1)} %copy-done.6, f32[16,16,128]{2,1,0:T(8,128)S(1)} %copy-done.8, f32[16,16,128]{2,1,0:T(8,128)S(1)} %copy-done.4, f32[256,128]{1,0:T(8,128)S(1)} %bitcast.7, f32[256,128]{1,0:T(8,128)S(1)} %bitcast.8, bf16[4352,512]{1,0:T(8,128)(2,1)S(1)} %bitcast.6, ...), custom_call_target="tpu_custom_call" | custom-call | tf_op jit(solution)/shard_map/pallas_call | solution.py:246
  (40 shorter events, 4.5 us)
Async XLA Ops:
  4.1 22.4 %collective-permute-start.1 = (f32[216,128]{1,0:T(8,128)}, f32[216,128]{1,0:T(8,128)S(1)}, u32[]{:S(2)}, u32[]{:S(2)}) collective-permute-start(f32[216,128]{1,0:T(8,128)} %get-tuple-element.16.down_ref), channel_id=1, source_target_pairs={{1,0},{2,1},{3,2},{4,3},{5,4},{6,5},{7,6},{8,7},{9,8},{10,9},{11,1... | collective-permute-start | bytes 331784 | tf_op jit(solution)/shard_map/ppermute | solution.py:200
  14.4 12.1 %collective-permute-start = (f32[16,8,128]{2,1,0:T(8,128)}, f32[16,8,128]{2,1,0:T(8,128)S(1)}, u32[]{:S(2)}, u32[]{:S(2)}) collective-permute-start(f32[16,8,128]{2,1,0:T(8,128)} %get-tuple-element.15), channel_id=1, source_target_pairs={{0,1},{1,2},{2,3},{3,4},{4,5},{5,6},{6,7},{7,8},{8,9},{9,10},{10,1... | collective-permute-start | bytes 196616 | tf_op jit(solution)/shard_map/ppermute | solution.py:200
  29.1 9.0 %collective-permute-start.3 = (f32[432,128]{1,0:T(8,128)}, f32[432,128]{1,0:T(8,128)S(1)}, u32[]{:S(2)}, u32[]{:S(2)}) collective-permute-start(f32[432,128]{1,0:T(8,128)} %get-tuple-element.19), channel_id=1, source_target_pairs={{32,0},{64,32},{96,64},{128,96},{160,128},{192,160},{224,192},{33,... | collective-permute-start | bytes 663560 | tf_op jit(solution)/shard_map/ppermute | solution.py:200
  33.2 4.9 %collective-permute-start.2 = (f32[8,32,128]{2,1,0:T(8,128)}, f32[8,32,128]{2,1,0:T(8,128)S(1)}, u32[]{:S(2)}, u32[]{:S(2)}) collective-permute-start(f32[8,32,128]{2,1,0:T(8,128)} %get-tuple-element.18), channel_id=1, source_target_pairs={{0,32},{32,64},{64,96},{96,128},{128,160},{160,192},{192,224},{1,3... | collective-permute-start | bytes 393224 | tf_op jit(solution)/shard_map/ppermute | solution.py:200
  38.1 0.9 copy-start.5
  39.0 0.9 copy-start.7
  39.9 0.9 copy-start.9
  40.8 0.9 copy-start.11
  41.7 0.9 %copy-start.13 = (f32[16,32,128]{2,1,0:T(8,128)S(1)}, f32[16,32,128]{2,1,0:T(8,128)}, u32[]{:S(2)}) copy-start(f32[16,32,128]{2,1,0:T(8,128)} %get-tuple-element.17.wide_ref) | copy-start | bytes 786436
  51.5 3.5 %copy-start = (bf16[4352,1024]{1,0:T(8,128)(2,1)}, bf16[4352,1024]{1,0:T(8,128)(2,1)S(1)}, u32[]{:S(2)}) copy-start(bf16[4352,1024]{1,0:T(8,128)(2,1)S(1)} %get-tuple-element.25.wa_ref) | copy-start | bytes 26738692
  54.9 2.2 %copy-start.2 = (bf16[4352,512]{1,0:T(8,128)(2,1)}, bf16[4352,512]{1,0:T(8,128)(2,1)S(1)}, u32[]{:S(2)}) copy-start(bf16[4352,512]{1,0:T(8,128)(2,1)S(1)} %get-tuple-element.23.wb_ref) | copy-start | bytes 13369348
  57.1 14.3 %copy-start.3 = (f32[16,16,128]{2,1,0:T(8,128)}, f32[16,16,128]{2,1,0:T(8,128)S(1)}, u32[]{:S(2)}) copy-start(f32[16,16,128]{2,1,0:T(8,128)S(1)} %get-tuple-element.20.v_ref) | copy-start | bytes 393220
  57.1 31.8 %slice-start = ((s8[4456448]{0:T(1024)(128)(4,1)}), s8[262144]{0:T(1024)(128)(4,1)S(1)}, s32[]{:S(2)}) async-start(s8[4456448]{0:T(1024)(128)(4,1)} %bitcast.5), calls=%async_computation | async-start | bytes 524288
  57.1 12.8 %collective-permute-start.4 = (f32[16,8,128]{2,1,0:T(8,128)S(1)}, f32[16,8,128]{2,1,0:T(8,128)S(1)}, u32[]{:S(2)}, u32[]{:S(2)}) collective-permute-start(f32[16,8,128]{2,1,0:T(8,128)S(1)} %get-tuple-element.27), channel_id=1, source_target_pairs={{0,1},{1,2},{2,3},{3,4},{4,5},{5,6},{6,7},{7,8},{8,9},{9,10},{10,1... | collective-permute-start | bytes 196616 | tf_op jit(solution)/shard_map/ppermute | solution.py:200
  59.5 11.9 %collective-permute-start.5 = (f32[16,8,128]{2,1,0:T(8,128)S(1)}, f32[16,8,128]{2,1,0:T(8,128)S(1)}, u32[]{:S(2)}, u32[]{:S(2)}) collective-permute-start(f32[16,8,128]{2,1,0:T(8,128)S(1)} %get-tuple-element.26), channel_id=1, source_target_pairs={{1,0},{2,1},{3,2},{4,3},{5,4},{6,5},{7,6},{8,7},{9,8},{10,9},{11,1... | collective-permute-start | bytes 196616 | tf_op jit(solution)/shard_map/ppermute | solution.py:200
  69.9 1.5 %copy-start.15 = (f32[16,8,128]{2,1,0:T(8,128)}, f32[16,8,128]{2,1,0:T(8,128)S(1)}, u32[]{:S(2)}) copy-start(f32[16,8,128]{2,1,0:T(8,128)S(1)} %collective-permute-done.4.before_ref) | copy-start | bytes 196612
  73.7 15.1 %collective-permute-start.6 = (f32[8,32,128]{2,1,0:T(8,128)}, f32[8,32,128]{2,1,0:T(8,128)S(1)}, u32[]{:S(2)}, u32[]{:S(2)}) collective-permute-start(f32[8,32,128]{2,1,0:T(8,128)} %get-tuple-element.21), channel_id=1, source_target_pairs={{0,32},{32,64},{64,96},{96,128},{128,160},{160,192},{192,224},{1,3... | collective-permute-start | bytes 393224 | tf_op jit(solution)/shard_map/ppermute | solution.py:200
  79.9 8.9 %collective-permute-start.7 = (f32[8,32,128]{2,1,0:T(8,128)}, f32[8,32,128]{2,1,0:T(8,128)S(1)}, u32[]{:S(2)}, u32[]{:S(2)}) collective-permute-start(f32[8,32,128]{2,1,0:T(8,128)} %get-tuple-element.22), channel_id=1, source_target_pairs={{32,0},{64,32},{96,64},{128,96},{160,128},{192,160},{224,192},{33,... | collective-permute-start | bytes 393224 | tf_op jit(solution)/shard_map/ppermute | solution.py:200
  81.8 3.5 %copy-start.1 = (bf16[4352,1024]{1,0:T(8,128)(2,1)S(1)}, bf16[4352,1024]{1,0:T(8,128)(2,1)}, u32[]{:S(2)}) copy-start(bf16[4352,1024]{1,0:T(8,128)(2,1)} %copy-done) | copy-start | bytes 26738692
  85.4 0.9 %copy-start.12 = (f32[16,32,128]{2,1,0:T(8,128)S(1)}, f32[16,32,128]{2,1,0:T(8,128)}, u32[]{:S(2)}) copy-start(f32[16,32,128]{2,1,0:T(8,128)} %get-tuple-element.24.wide_ref) | copy-start | bytes 786436
  86.3 2.5 %slice-start.1 = ((s8[4456448]{0:T(1024)(128)(4,1)}), s8[4194304]{0:T(1024)(128)(4,1)S(1)}, s32[]{:S(2)}) async-start(s8[4456448]{0:T(1024)(128)(4,1)} %bitcast.5), calls=%async_computation.1 | async-start | bytes 8388608
  86.3 2.5 %copy-start.4 = (f32[16,16,128]{2,1,0:T(8,128)S(1)}, f32[16,16,128]{2,1,0:T(8,128)}, u32[]{:S(2)}) copy-start(f32[16,16,128]{2,1,0:T(8,128)} %copy-done.3) | copy-start | bytes 393220
  86.3 2.6 %copy-start.6 = (f32[16,16,128]{2,1,0:T(8,128)S(1)}, f32[16,16,128]{2,1,0:T(8,128)}, u32[]{:S(2)}) copy-start(f32[16,16,128]{2,1,0:T(8,128)} %d_ref.5) | copy-start | bytes 393220
  86.3 2.6 %copy-start.8 = (f32[16,16,128]{2,1,0:T(8,128)S(1)}, f32[16,16,128]{2,1,0:T(8,128)}, u32[]{:S(2)}) copy-start(f32[16,16,128]{2,1,0:T(8,128)} %p_ref.5) | copy-start | bytes 393220
  (3 other events, 1.9 us)
where the time goes:
time: 92.1 us; the launch traced here: 91 us
  starting transfers between devices  39.4 us (43%)
  Pallas kernels  18.9 us (21%)
  local copies, waits for them, and re-layouts  17.6 us (19%)
  waiting for transfers between devices  14.3 us (16%)
    ppermute x8, starting transfers between devices, passed_along(): lax.ppermute(shard, axis, [(i, i + by) for i in range(length) if 0 <= i +...  39.4 us
    unnamed x39, local copies, waits for them, and re-layouts  17.6 us
    ppermute x8, waiting for transfers between devices, passed_along(): lax.ppermute(shard, axis, [(i, i + by) for i in range(length) if 0 <= i +...  14.3 us
    pallas_call x1, Pallas kernels, local(): pl.pallas_call(step_one, out_shape=(pinned((ROWS, 1024), jnp.bfloat16), p...  8.81 us
    pallas_call x1, Pallas kernels, local(): pl.pallas_call(step_two_inner, out_shape=pinned((ROWS, Z), jnp.float32),...  2.49 us
    pallas_call x1, Pallas kernels, local(): pl.pallas_call(step_two_outer, out_shape=(f32(T, T, Z), f32(T, T, Z)), in...  2.12 us
    pallas_call x1, Pallas kernels, local(): call(pack_first, (f32(T, GROUP, Z), f32(H, GROUP, Z), f32(H * GROUP + 2 *...  1.91 us
    pallas_call x1, Pallas kernels, local(): call(prepare, (f32(T, T, Z), f32(T, H, Z), f32(T * H + PACKED, Z)), [pltp...  1.87 us
  transfers between devices with their start and end apart: 8, of which 4 were waited for; matrix products, arithmetic and copies ran while one was open for 0% of the time, Pallas kernels for 3%

commit v1 on v0

v1 whole, which is shorter than its diff:
```python
import jax
import jax.numpy as jnp
from jax import lax
from jax.experimental import pallas as pl
from jax.experimental.pallas import tpu as pltpu
from jax.sharding import PartitionSpec as P

ITERS = 2
relaxation = 0.7

H = 8
TAPS = 17
T = 16
Z = 128
GROUP = 32
SPAN = 640
ROWS = 2 * TAPS * 8 * T
PACKED = 88
VMEM = pl.BlockSpec(memory_space=pltpu.VMEM)
MIB = 1 << 20


def held(*shape, dtype=jnp.float32):
    return pltpu.VMEM(shape, dtype)


def keep(x):
    return pltpu.with_memory_space_constraint(x, pltpu.VMEM)


def call(kernel, outs, mib, scratch=()):
    def run(*operands):
        return pl.pallas_call(
            kernel,
            out_shape=outs,
            in_specs=[VMEM] * len(operands),
            out_specs=jax.tree.map(lambda _: VMEM, outs),
            scratch_shapes=list(scratch),
            compiler_params=pltpu.CompilerParams(vmem_limit_bytes=int(mib * MIB)),
        )(*operands)

    return run


def even(axis):
    return lax.axis_index(axis) % 2 == 0


def last(axis):
    return lax.axis_index(axis) == lax.axis_size(axis) - 1


def swapped(axis, first, second):
    size = lax.axis_size(axis)
    received = []
    for start, sent in ((0, first), (1, second)):
        pairs = []
        for i in range(start, size - 1, 2):
            pairs += [(i, i + 1), (i + 1, i)]
        received.append(lax.ppermute(sent, axis, pairs))
    return received


def by_parity(axis, action):
    pl.when(even(axis))(lambda: action(0, 1))
    pl.when(jnp.logical_not(even(axis)))(lambda: action(1, 0))


def f32(*shape):
    return jax.ShapeDtypeStruct(shape, jnp.float32)


def prepare(d_ref, p_ref, psf_ref, v_ref, first_ref, second_ref, d_out_ref, p_out_ref, t_ref):
    d_out_ref[...] = d_ref[...]
    p_out_ref[...] = p_ref[...]
    v = d_ref[...] * p_ref[...]
    v_ref[...] = v
    t_ref[...] = jnp.zeros_like(t_ref)
    for a in range(TAPS):
        t_ref[GROUP * a : GROUP * a + TAPS, :TAPS] = psf_ref[0, 0, a]
    turned = t_ref[...].T
    sent = (first_ref, second_ref)
    for ref in sent:
        for u in range(5):
            ref[T * H + u * TAPS : T * H + (u + 1) * TAPS, :] = turned[:TAPS, u * 128 : (u + 1) * 128]
        ref[T * H + 5 * TAPS :, :] = jnp.zeros((PACKED - 5 * TAPS, Z), jnp.float32)

    def place(onward, back):
        sent[onward][: T * H, :] = v_ref[:, H:, :].reshape(T * H, Z)
        sent[back][: T * H, :] = v_ref[:, :H, :].reshape(T * H, Z)

    by_parity("gy", place)


def widen(v_ref, arrived, wide_ref):
    wide_ref[:, H : H + T, :] = v_ref[...]

    def place(onward, back):
        wide_ref[:, :H, :] = arrived[back][: T * H, :].reshape(T, H, Z)
        wide_ref[:, H + T :, :] = arrived[onward][: T * H, :].reshape(T, H, Z)

    by_parity("gy", place)


def pack_first(v_ref, own_ref, a_ref, b_ref, wide_ref, first_ref, second_ref):
    widen(v_ref, (a_ref, b_ref), wide_ref)
    sent = (first_ref, second_ref)
    side = H * GROUP

    def kernels(onward, back):
        for ref in sent:
            ref[side : side + PACKED, :] = own_ref[T * H :, :]
            ref[side + PACKED :, :] = jnp.where(last("gy"), own_ref[T * H :, :], (a_ref, b_ref)[onward][T * H :, :])

    by_parity("gy", kernels)

    def place(onward, back):
        sent[onward][:side, :] = wide_ref[H:].reshape(side, Z)
        sent[back][:side, :] = wide_ref[:H].reshape(side, Z)

    by_parity("gx", place)


def pack_next(v_ref, a_ref, b_ref, wide_ref, first_ref, second_ref):
    widen(v_ref, (a_ref, b_ref), wide_ref)
    sent = (first_ref, second_ref)
    side = H * GROUP

    def place(onward, back):
        sent[onward][...] = wide_ref[H:].reshape(side, Z)
        sent[back][...] = wide_ref[:H].reshape(side, Z)

    by_parity("gx", place)


def halves(v):
    high = v.astype(jnp.bfloat16)
    low = (v - high.astype(jnp.float32)).astype(jnp.bfloat16)
    return jnp.concatenate([high, low], axis=1)


def stationary(v):
    both = halves(v)
    return jnp.concatenate([both, both], axis=0)


def slot(term, m, r, u):
    return ((term * 2 + m) * 4 + r) * 5 + u


def spread(ref, at):
    return jnp.concatenate([ref[at + u * TAPS : at + (u + 1) * TAPS, :] for u in range(5)], axis=1)


def build(mine_ref, arrived, wa_ref, wb_ref, rows_ref):
    side = H * GROUP
    own, nexty = spread(mine_ref, side), spread(mine_ref, side + PACKED)
    onward = [jnp.where(even("gx"), spread(arrived[0], side + k * PACKED), spread(arrived[1], side + k * PACKED)) for k in range(2)]
    nextx, corner = jnp.where(last("gx"), own, onward[0]), jnp.where(last("gx"), nexty, onward[1])
    for m, (near, far) in enumerate(((own, nexty), (nextx, corner))):
        for term, table in enumerate((near, far - near)):
            for r in range(4):
                rolled = table if r == 0 else pltpu.roll(table, GROUP * r, 1)
                for u in range(5):
                    rows_ref[slot(term, m, r, u), :TAPS, :] = rolled[:, u * 128 : (u + 1) * 128]
    along = lax.broadcasted_iota(jnp.int32, (H, Z), 0).astype(jnp.float32)
    steps = [(along + (0.5 + H * half)) / T for half in range(2)]
    zero = jnp.zeros((T, 128), jnp.bfloat16)

    @pl.loop(0, TAPS)
    def _(c):
        def base(x):
            return pl.multiple_of((((x // 8) * TAPS + c) * 8 + x % 8) * T, T)

        for r in range(4):
            for u in range(5):
                node = []
                for m in range(2):
                    near = rows_ref[slot(0, m, r, u), pl.ds(c, H, stride=0), :]
                    step = rows_ref[slot(1, m, r, u), pl.ds(c, H, stride=0), :]
                    node.append(
                        jnp.concatenate(
                            [
                                pltpu.roll(near + steps[half] * step, H * half, 1, stride=1, stride_axis=0)
                                for half in range(2)
                            ],
                            axis=0,
                        )
                    )
                across = node[1] - node[0]
                for q in range(4):
                    x = 4 * q + r
                    w = node[0] + ((x + 0.5) / T) * across
                    high = w.astype(jnp.bfloat16)
                    low = (w - high.astype(jnp.float32)).astype(jnp.bfloat16)
                    tile = q + u
                    if 2 <= tile < 6:
                        wa_ref[pl.ds(base(x), T), (tile - 2) * 128 : (tile - 1) * 128] = high
                        wa_ref[pl.ds(base(x), T), 512 + (tile - 2) * 128 : 512 + (tile - 1) * 128] = low
                    else:
                        at = (tile % 2) * 128
                        wb_ref[pl.ds(base(x), T), at : at + 128] = high
                        wb_ref[pl.ds(base(x), T), 256 + at : 256 + at + 128] = low
            for q, ref, at, width in ((0, wa_ref, 384, 512), (1, wb_ref, 0, 256), (2, wb_ref, 128, 256), (3, wa_ref, 0, 512)):
                ref[pl.ds(base(4 * q + r), T), at : at + 128] = zero
                ref[pl.ds(base(4 * q + r), T), width + at : width + at + 128] = zero


def product(w, v):
    both = jnp.dot(w, v, preferred_element_type=jnp.float32)
    return both[:, :Z] + both[:, Z:]


def inner_part(wide_ref, wa_ref, r_ref):
    v = stationary(wide_ref[...].reshape(T * GROUP, Z))
    for h in range(2):
        rows = slice(h * TAPS * 128, (h + 1) * TAPS * 128)
        r_ref[rows, :] = product(wa_ref[rows, :], v)


def outer_part(arrived, wb_ref, r_ref, out_ref, side_ref):
    lane = lax.broadcasted_iota(jnp.int32, (128, Z), 1)

    def place(onward, back):
        side_ref[0] = arrived[back][: H * GROUP, :]
        side_ref[1] = arrived[onward][: H * GROUP, :]

    by_parity("gx", place)
    for h in range(2):
        v = stationary(side_ref[h])
        total = None
        for c in range(TAPS):
            at = slice((h * TAPS + c) * 128, (h * TAPS + c + 1) * 128)
            part = r_ref[at, :] + product(wb_ref[at, :], v)
            if c != H:
                part = pltpu.roll(part, (H - c) % Z, 1)
                part = jnp.where((lane >= H - c) & (lane < Z + H - c), part, 0.0)
            total = part if total is None else total + part
        out_ref[h * 8 : (h + 1) * 8] = total.reshape(8, T, Z)


def step_one(d_ref, p_ref, wide_ref, mine_ref, a_ref, b_ref,
             wa_ref, wb_ref, model_ref, first_ref, second_ref, rows_ref, r_ref, k_ref, side_ref):
    build(mine_ref, (a_ref, b_ref), wa_ref, wb_ref, rows_ref)
    inner_part(wide_ref, wa_ref, r_ref)
    outer_part((a_ref, b_ref), wb_ref, r_ref, k_ref, side_ref)
    v = wide_ref[:, H : H + T, :]
    residual = d_ref[...] - (v + k_ref[...])
    model_ref[...] = v + relaxation * p_ref[...] * residual
    sent = (first_ref, second_ref)

    def place(onward, back):
        sent[onward][...] = model_ref[:, H:, :].reshape(T * H, Z)
        sent[back][...] = model_ref[:, :H, :].reshape(T * H, Z)

    by_parity("gy", place)


def step_two(d_ref, p_ref, v_ref, a_ref, b_ref, wb_ref, r_ref, model_ref, residual_ref, k_ref, side_ref):
    outer_part((a_ref, b_ref), wb_ref, r_ref, k_ref, side_ref)
    v = v_ref[...]
    residual = d_ref[...] - (v + k_ref[...])
    residual_ref[...] = residual
    model_ref[...] = v + relaxation * p_ref[...] * residual


def local(data, precond, psf):
    side = H * GROUP
    wide_shape = held(T, GROUP, Z)
    block = pltpu.VMEM((T, T, Z), jnp.float32)
    sides = pltpu.VMEM((2, side, Z), jnp.float32)
    row = held(T * H + PACKED, Z)
    tile = held(T, T, Z)
    v, first, second, data, precond = call(prepare, (tile, row, row, tile, tile), 4, [pltpu.VMEM((SPAN, 128), jnp.float32)])(
        data, precond, psf
    )
    a, b = swapped("gy", first, second)
    row = held(side + 2 * PACKED, Z)
    wide, first, second = call(pack_first, (wide_shape, row, row), 3)(*map(keep, (v, first, a, b)))
    a, b = swapped("gx", first, second)
    row = held(T * H, Z)
    wa, wb, v, first, second = call(
        step_one,
        (held(ROWS, 1024, dtype=jnp.bfloat16), held(ROWS, 512, dtype=jnp.bfloat16), held(T, T, Z), row, row),
        14,
        [pltpu.VMEM((80, 24, 128), jnp.float32), pltpu.VMEM((ROWS, Z), jnp.float32), block, sides],
    )(*map(keep, (data, precond, wide, first, a, b)))
    a, b = swapped("gy", first, second)
    row = held(side, Z)
    wide, first, second = call(pack_next, (wide_shape, row, row), 3)(*map(keep, (v, a, b)))
    a, b = swapped("gx", first, second)
    part = call(inner_part, held(ROWS, Z), 8)(*map(keep, (wide, wa)))
    return call(step_two, (f32(T, T, Z), f32(T, T, Z)), 6, [block, sides])(
        *map(keep, (data, precond, v, a, b, wb, part))
    )


def solution(mesh):
    placed = (P("gx", "gy", None), P("gx", "gy", None), P("gx", "gy", None, None, None))
    return jax.shard_map(
        local,
        mesh=mesh,
        in_specs=placed,
        out_specs=(P("gx", "gy", None), P("gx", "gy", None)),
        check_vma=False,
    )
```

time: 92.1 us -> 65.8 us (0.71)
  local copies, waits for them, and re-layouts: 17.6 us -> 2.73 us
  starting transfers between devices: 39.4 us -> 26.8 us
  waiting for transfers between devices: 14.3 us -> 21.9 us
  Pallas kernels: 18.9 us -> 13.4 us
    unnamed x39 -> x5, local copies, waits for them, and re-layouts: 17.6 us -> 2.73 us
    ppermute x8, starting transfers between devices: 39.4 us -> 26.8 us  [swapped(): received.append(lax.ppermute(sent, axis, pairs))]
    ppermute x8, waiting for transfers between devices: 14.3 us -> 21.9 us  [swapped(): received.append(lax.ppermute(sent, axis, pairs))]
    pallas_call x6, Pallas kernels: 18.9 us -> 13.4 us  [run(): pl.pallas_call(kernel, out_shape=outs, in_specs=[VMEM] * len(operands), o...]
  transfers between devices with their start and end apart: 8 -> 8, of which waited for: 4 -> 4; matrix products, arithmetic and copies ran while one was open for 0% -> 0% of each run, Pallas kernels for 3% -> 4%
where the time goes in v1:
time: 65.8 us; the launch traced here: 65.5 us
  starting transfers between devices  26.8 us (41%)
  waiting for transfers between devices  21.9 us (33%)
  Pallas kernels  13.4 us (20%)
  local copies, waits for them, and re-layouts  2.73 us (4%)
  between operations  0.73 us (1%)
    ppermute x8, starting transfers between devices, swapped(): received.append(lax.ppermute(sent, axis, pairs))  26.8 us
    ppermute x8, waiting for transfers between devices, swapped(): received.append(lax.ppermute(sent, axis, pairs))  21.9 us
    pallas_call x6, Pallas kernels, run(): pl.pallas_call(kernel, out_shape=outs, in_specs=[VMEM] * len(operands), o...  13.4 us
    unnamed x5, local copies, waits for them, and re-layouts  2.73 us
  transfers between devices with their start and end apart: 8, of which 4 were waited for; matrix products, arithmetic and copies ran while one was open for 0% of the time, Pallas kernels for 4%

profile of v1, /device:TPU:57, one launch (start us, length us, event | category | flops | bytes accessed | tf_op | source)
XLA Modules:
  0.0 65.5 jit_solution(17248059855390817864)
XLA Ops:
  0.6 0.9 %copy.5.psf_ref = f32[1,1,17,17,17]{4,3,2,1,0:T(8,128)S(1)} copy(f32[1,1,17,17,17]{4,1,3,2,0:T(1,128)} %param.5) | data formatting | bytes 39304 | tf_op args[2]
  1.6 0.0 copy-start
  1.6 0.9 %copy-done = f32[16,16,128]{2,1,0:T(8,128)S(1)} copy-done((f32[16,16,128]{2,1,0:T(8,128)S(1)}, f32[16,16,128]{2,1,0:T(8,128)}, u32[]{:S(2)}) %copy-start) | copy-done | bytes 131096
  2.5 0.9 %copy-done.1 = f32[16,16,128]{2,1,0:T(8,128)S(1)} copy-done((f32[16,16,128]{2,1,0:T(8,128)S(1)}, f32[16,16,128]{2,1,0:T(8,128)}, u32[]{:S(2)}) %copy-start.1) | copy-done | bytes 131096
  3.4 0.2 shard_map.50
  3.5 6.1 %collective-permute-start = (f32[216,128]{1,0:T(8,128)S(1)}, f32[216,128]{1,0:T(8,128)S(1)}, u32[]{:S(2)}, u32[]{:S(2)}) collective-permute-start(f32[216,128]{1,0:T(8,128)S(1)} %get-tuple-element.21.own_ref), channel_id=1, source_target_pairs={{0,1},{1,0},{2,3},{3,2},{4,5},{5,4},{6,7},{7,6},{8,9},{9,8},{10,11... | collective-permute-start | bytes 331784 | tf_op jit(solution)/shard_map/ppermute | solution.py:60
  9.6 4.3 %collective-permute-start.1 = (f32[216,128]{1,0:T(8,128)S(1)}, f32[216,128]{1,0:T(8,128)S(1)}, u32[]{:S(2)}, u32[]{:S(2)}) collective-permute-start(f32[216,128]{1,0:T(8,128)S(1)} %get-tuple-element.22), channel_id=1, source_target_pairs={{1,2},{2,1},{3,4},{4,3},{5,6},{6,5},{7,8},{8,7},{9,10},{10,9},{11,... | collective-permute-start | bytes 331784 | tf_op jit(solution)/shard_map/ppermute | solution.py:60
  14.0 0.0 collective-permute-done.a_ref
  14.0 10.9 %collective-permute-done.1.b_ref = f32[216,128]{1,0:T(8,128)S(1)} collective-permute-done((f32[216,128]{1,0:T(8,128)S(1)}, f32[216,128]{1,0:T(8,128)S(1)}, u32[]{:S(2)}, u32[]{:S(2)}) %collective-permute-start.1) | collective-permute-done | bytes 110624 | tf_op jit(solution)/shard_map/ppermute | solution.py:60
  24.9 0.1 shard_map.51
  25.0 1.5 %collective-permute-start.2 = (f32[432,128]{1,0:T(8,128)S(1)}, f32[432,128]{1,0:T(8,128)S(1)}, u32[]{:S(2)}, u32[]{:S(2)}) collective-permute-start(f32[432,128]{1,0:T(8,128)S(1)} %get-tuple-element.24.mine_ref), channel_id=1, source_target_pairs={{0,32},{32,0},{64,96},{96,64},{128,160},{160,128},{192,224},{224,1... | collective-permute-start | bytes 663560 | tf_op jit(solution)/shard_map/ppermute | solution.py:60
  26.5 2.7 %collective-permute-start.3 = (f32[432,128]{1,0:T(8,128)S(1)}, f32[432,128]{1,0:T(8,128)S(1)}, u32[]{:S(2)}, u32[]{:S(2)}) collective-permute-start(f32[432,128]{1,0:T(8,128)S(1)} %get-tuple-element.25), channel_id=1, source_target_pairs={{32,64},{64,32},{96,128},{128,96},{160,192},{192,160},{33,65},{65,... | collective-permute-start | bytes 663560 | tf_op jit(solution)/shard_map/ppermute | solution.py:60
  29.2 0.0 collective-permute-done.2.a_ref
  29.2 4.5 %collective-permute-done.3.b_ref = f32[432,128]{1,0:T(8,128)S(1)} collective-permute-done((f32[432,128]{1,0:T(8,128)S(1)}, f32[432,128]{1,0:T(8,128)S(1)}, u32[]{:S(2)}, u32[]{:S(2)}) %collective-permute-start.3) | collective-permute-done | bytes 221216 | tf_op jit(solution)/shard_map/ppermute | solution.py:60
  33.7 8.3 %shard_map.52 = (bf16[4352,1024]{1,0:T(8,128)(2,1)S(1)}, bf16[4352,512]{1,0:T(8,128)(2,1)S(1)}, f32[16,16,128]{2,1,0:T(8,128)S(1)}, f32[128,128]{1,0:T(8,128)S(1)}, f32[128,128]{1,0:T(8,128)S(1)}) custom-call(f32[16,16,128]{2,1,0:T(8,128)S(1)} %get-tuple-element.18.d_ref, f32[16,16,128]{2,1,0:T(8,128)S(1)} %get-tuple-element.19.p_ref, ...), custom_call_target="tpu_custom_call" | custom-call | tf_op jit(solution)/shard_map/pallas_call | solution.py:33
  42.0 0.9 %collective-permute-start.4 = (f32[128,128]{1,0:T(8,128)S(1)}, f32[128,128]{1,0:T(8,128)S(1)}, u32[]{:S(2)}, u32[]{:S(2)}) collective-permute-start(f32[128,128]{1,0:T(8,128)S(1)} %get-tuple-element.27), channel_id=1, source_target_pairs={{0,1},{1,0},{2,3},{3,2},{4,5},{5,4},{6,7},{7,6},{8,9},{9,8},{10,11... | collective-permute-start | bytes 196616 | tf_op jit(solution)/shard_map/ppermute | solution.py:60
  42.9 6.8 %collective-permute-start.5 = (f32[128,128]{1,0:T(8,128)S(1)}, f32[128,128]{1,0:T(8,128)S(1)}, u32[]{:S(2)}, u32[]{:S(2)}) collective-permute-start(f32[128,128]{1,0:T(8,128)S(1)} %get-tuple-element.28), channel_id=1, source_target_pairs={{1,2},{2,1},{3,4},{4,3},{5,6},{6,5},{7,8},{8,7},{9,10},{10,9},{11,... | collective-permute-start | bytes 196616 | tf_op jit(solution)/shard_map/ppermute | solution.py:60
  49.7 5.1 %collective-permute-done.5.b_ref = f32[128,128]{1,0:T(8,128)S(1)} collective-permute-done((f32[128,128]{1,0:T(8,128)S(1)}, f32[128,128]{1,0:T(8,128)S(1)}, u32[]{:S(2)}, u32[]{:S(2)}) %collective-permute-start.5) | collective-permute-done | bytes 65568 | tf_op jit(solution)/shard_map/ppermute | solution.py:60
  54.8 0.1 shard_map.53
  54.9 2.2 %collective-permute-start.6 = (f32[256,128]{1,0:T(8,128)S(1)}, f32[256,128]{1,0:T(8,128)S(1)}, u32[]{:S(2)}, u32[]{:S(2)}) collective-permute-start(f32[256,128]{1,0:T(8,128)S(1)} %get-tuple-element.29), channel_id=1, source_target_pairs={{0,32},{32,0},{64,96},{96,64},{128,160},{160,128},{192,224},{224,1... | collective-permute-start | bytes 393224 | tf_op jit(solution)/shard_map/ppermute | solution.py:60
  57.1 2.3 %collective-permute-start.7 = (f32[256,128]{1,0:T(8,128)S(1)}, f32[256,128]{1,0:T(8,128)S(1)}, u32[]{:S(2)}, u32[]{:S(2)}) collective-permute-start(f32[256,128]{1,0:T(8,128)S(1)} %get-tuple-element.30), channel_id=1, source_target_pairs={{32,64},{64,32},{96,128},{128,96},{160,192},{192,160},{33,65},{65,... | collective-permute-start | bytes 393224 | tf_op jit(solution)/shard_map/ppermute | solution.py:60
  59.4 2.6 %shard_map.54.r_ref = f32[4352,128]{1,0:T(8,128)S(1)} custom-call(f32[16,32,128]{2,1,0:T(8,128)S(1)} %get-tuple-element.32.wide_ref, bf16[4352,1024]{1,0:T(8,128)(2,1)S(1)} %get-tuple-element.33.wa_ref), custom_call_target="tpu_custom_call" | custom-call | tf_op jit(solution)/shard_map/pallas_call | solution.py:33
  62.1 1.3 %collective-permute-done.7.b_ref = f32[256,128]{1,0:T(8,128)S(1)} collective-permute-done((f32[256,128]{1,0:T(8,128)S(1)}, f32[256,128]{1,0:T(8,128)S(1)}, u32[]{:S(2)}, u32[]{:S(2)}) %collective-permute-start.7) | collective-permute-done | bytes 131104 | tf_op jit(solution)/shard_map/ppermute | solution.py:60
  63.4 2.1 %shard_map.55 = (f32[16,16,128]{2,1,0:T(8,128)}, f32[16,16,128]{2,1,0:T(8,128)}) custom-call(f32[16,16,128]{2,1,0:T(8,128)S(1)} %get-tuple-element.18.d_ref, f32[16,16,128]{2,1,0:T(8,128)S(1)} %get-tuple-element.19.p_ref, f32[16,16,128]{2,1,0:T(8,128)S(1)} %get-tuple-element.26.v_ref, f32[256,128]{1,0:T(8,128)S(1)} %collective-permute-done.6.a_ref, ...), custom_call_target="tpu_custom_call" | custom-call | tf_op jit(solution)/shard_map/pallas_call | solution.py:33
  (3 shorter events, 0.0 us)
Async XLA Ops:
  1.6 0.9 %copy-start = (f32[16,16,128]{2,1,0:T(8,128)S(1)}, f32[16,16,128]{2,1,0:T(8,128)}, u32[]{:S(2)}) copy-start(f32[16,16,128]{2,1,0:T(8,128)} %d_ref.1) | copy-start | bytes 393220
  2.5 0.9 %copy-start.1 = (f32[16,16,128]{2,1,0:T(8,128)S(1)}, f32[16,16,128]{2,1,0:T(8,128)}, u32[]{:S(2)}) copy-start(f32[16,16,128]{2,1,0:T(8,128)} %p_ref.1) | copy-start | bytes 393220
  3.5 10.4 %collective-permute-start = (f32[216,128]{1,0:T(8,128)S(1)}, f32[216,128]{1,0:T(8,128)S(1)}, u32[]{:S(2)}, u32[]{:S(2)}) collective-permute-start(f32[216,128]{1,0:T(8,128)S(1)} %get-tuple-element.21.own_ref), channel_id=1, source_target_pairs={{0,1},{1,0},{2,3},{3,2},{4,5},{5,4},{6,7},{7,6},{8,9},{9,8},{10,11... | collective-permute-start | bytes 331784 | tf_op jit(solution)/shard_map/ppermute | solution.py:60
  9.6 15.2 %collective-permute-start.1 = (f32[216,128]{1,0:T(8,128)S(1)}, f32[216,128]{1,0:T(8,128)S(1)}, u32[]{:S(2)}, u32[]{:S(2)}) collective-permute-start(f32[216,128]{1,0:T(8,128)S(1)} %get-tuple-element.22), channel_id=1, source_target_pairs={{1,2},{2,1},{3,4},{4,3},{5,6},{6,5},{7,8},{8,7},{9,10},{10,9},{11,... | collective-permute-start | bytes 331784 | tf_op jit(solution)/shard_map/ppermute | solution.py:60
  25.0 4.2 %collective-permute-start.2 = (f32[432,128]{1,0:T(8,128)S(1)}, f32[432,128]{1,0:T(8,128)S(1)}, u32[]{:S(2)}, u32[]{:S(2)}) collective-permute-start(f32[432,128]{1,0:T(8,128)S(1)} %get-tuple-element.24.mine_ref), channel_id=1, source_target_pairs={{0,32},{32,0},{64,96},{96,64},{128,160},{160,128},{192,224},{224,1... | collective-permute-start | bytes 663560 | tf_op jit(solution)/shard_map/ppermute | solution.py:60
  26.5 7.2 %collective-permute-start.3 = (f32[432,128]{1,0:T(8,128)S(1)}, f32[432,128]{1,0:T(8,128)S(1)}, u32[]{:S(2)}, u32[]{:S(2)}) collective-permute-start(f32[432,128]{1,0:T(8,128)S(1)} %get-tuple-element.25), channel_id=1, source_target_pairs={{32,64},{64,32},{96,128},{128,96},{160,192},{192,160},{33,65},{65,... | collective-permute-start | bytes 663560 | tf_op jit(solution)/shard_map/ppermute | solution.py:60
  42.0 7.6 %collective-permute-start.4 = (f32[128,128]{1,0:T(8,128)S(1)}, f32[128,128]{1,0:T(8,128)S(1)}, u32[]{:S(2)}, u32[]{:S(2)}) collective-permute-start(f32[128,128]{1,0:T(8,128)S(1)} %get-tuple-element.27), channel_id=1, source_target_pairs={{0,1},{1,0},{2,3},{3,2},{4,5},{5,4},{6,7},{7,6},{8,9},{9,8},{10,11... | collective-permute-start | bytes 196616 | tf_op jit(solution)/shard_map/ppermute | solution.py:60
  42.9 11.9 %collective-permute-start.5 = (f32[128,128]{1,0:T(8,128)S(1)}, f32[128,128]{1,0:T(8,128)S(1)}, u32[]{:S(2)}, u32[]{:S(2)}) collective-permute-start(f32[128,128]{1,0:T(8,128)S(1)} %get-tuple-element.28), channel_id=1, source_target_pairs={{1,2},{2,1},{3,4},{4,3},{5,6},{6,5},{7,8},{8,7},{9,10},{10,9},{11,... | collective-permute-start | bytes 196616 | tf_op jit(solution)/shard_map/ppermute | solution.py:60
  54.9 7.2 %collective-permute-start.6 = (f32[256,128]{1,0:T(8,128)S(1)}, f32[256,128]{1,0:T(8,128)S(1)}, u32[]{:S(2)}, u32[]{:S(2)}) collective-permute-start(f32[256,128]{1,0:T(8,128)S(1)} %get-tuple-element.29), channel_id=1, source_target_pairs={{0,32},{32,0},{64,96},{96,64},{128,160},{160,128},{192,224},{224,1... | collective-permute-start | bytes 393224 | tf_op jit(solution)/shard_map/ppermute | solution.py:60
  57.1 6.3 %collective-permute-start.7 = (f32[256,128]{1,0:T(8,128)S(1)}, f32[256,128]{1,0:T(8,128)S(1)}, u32[]{:S(2)}, u32[]{:S(2)}) collective-permute-start(f32[256,128]{1,0:T(8,128)S(1)} %get-tuple-element.30), channel_id=1, source_target_pairs={{32,64},{64,32},{96,128},{128,96},{160,192},{192,160},{33,65},{65,... | collective-permute-start | bytes 393224 | tf_op jit(solution)/shard_map/ppermute | solution.py:60

commit v2 on v1

v2 whole, which is shorter than its diff:
```python
import jax
import jax.numpy as jnp
from jax import lax
from jax.experimental import pallas as pl
from jax.experimental.pallas import tpu as pltpu
from jax.sharding import PartitionSpec as P


relaxation = 0.7

H = 8
TAPS = 17
T = 16
Z = 128
GROUP = 32
DENSE = TAPS * TAPS
ROWS = 2 * TAPS * 8 * T
PACKED = 40
FOLD = 40
VMEM = pl.BlockSpec(memory_space=pltpu.VMEM)
MIB = 1 << 20


def held(*shape, dtype=jnp.float32):
    return pltpu.VMEM(shape, dtype)


def keep(x):
    return pltpu.with_memory_space_constraint(x, pltpu.VMEM)


def call(kernel, outs, mib, scratch=(), space=VMEM):
    def run(*operands):
        return pl.pallas_call(
            kernel,
            out_shape=outs,
            in_specs=[space] * len(operands),
            out_specs=jax.tree.map(lambda _: VMEM, outs),
            scratch_shapes=list(scratch),
            compiler_params=pltpu.CompilerParams(vmem_limit_bytes=int(mib * MIB)),
        )(*operands)

    return run


def even(axis):
    return lax.axis_index(axis) % 2 == 0


def last(axis):
    return lax.axis_index(axis) == lax.axis_size(axis) - 1


def swapped(axis, first, second):
    size = lax.axis_size(axis)
    received = []
    for start, sent in ((0, first), (1, second)):
        pairs = []
        for i in range(start, size - 1, 2):
            pairs += [(i, i + 1), (i + 1, i)]
        received.append(lax.ppermute(sent, axis, pairs))
    return received


def by_parity(axis, action):
    pl.when(even(axis))(lambda: action(0, 1))
    pl.when(jnp.logical_not(even(axis)))(lambda: action(1, 0))


def f32(*shape):
    return jax.ShapeDtypeStruct(shape, jnp.float32)


def prepare(d_hbm, p_hbm, psf_hbm, v_ref, first_ref, second_ref, d_ref, p_ref, psf_ref, t_ref, sems):
    copies = [
        pltpu.make_async_copy(src, dst, sems.at[k])
        for k, (src, dst) in enumerate(((psf_hbm, psf_ref), (d_hbm, d_ref), (p_hbm, p_ref)))
    ]
    for copy in copies:
        copy.start()
    t_ref[DENSE:, :] = jnp.zeros((384 - DENSE, 128), jnp.float32)
    copies[0].wait()
    t_ref[:DENSE, :TAPS] = psf_ref[:, 0, :]
    turned = t_ref[...].T
    sent = (first_ref, second_ref)
    rest = turned[:TAPS, 256:]
    rest = jnp.where(lax.broadcasted_iota(jnp.int32, rest.shape, 1) < DENSE - 256, rest, 0.0)
    for ref in sent:
        at = T * H
        ref[at : at + TAPS, :] = turned[:TAPS, :128]
        ref[at + TAPS : at + 2 * TAPS, :] = turned[:TAPS, 128:256]
        ref[at + 34 : at + 40, :] = rest[:6] + pltpu.roll(rest, FOLD, 1)[6:12]
        ref[at + 34 : at + 39, :] += pltpu.roll(rest, 2 * FOLD, 1)[12:17]
    copies[1].wait()
    copies[2].wait()
    v_ref[...] = d_ref[...] * p_ref[...]

    def place(onward, back):
        sent[onward][: T * H, :] = v_ref[:, H:, :].reshape(T * H, Z)
        sent[back][: T * H, :] = v_ref[:, :H, :].reshape(T * H, Z)

    by_parity("gy", place)


def widen(v_ref, arrived, wide_ref):
    wide_ref[:, H : H + T, :] = v_ref[...]

    def place(onward, back):
        wide_ref[:, :H, :] = arrived[back][: T * H, :].reshape(T, H, Z)
        wide_ref[:, H + T :, :] = arrived[onward][: T * H, :].reshape(T, H, Z)

    by_parity("gy", place)


def pack_first(v_ref, own_ref, a_ref, b_ref, wide_ref, first_ref, second_ref):
    widen(v_ref, (a_ref, b_ref), wide_ref)
    sent = (first_ref, second_ref)
    side = H * GROUP

    def kernels(onward, back):
        for ref in sent:
            ref[side : side + PACKED, :] = own_ref[T * H :, :]
            ref[side + PACKED :, :] = jnp.where(last("gy"), own_ref[T * H :, :], (a_ref, b_ref)[onward][T * H :, :])

    by_parity("gy", kernels)

    def place(onward, back):
        sent[onward][:side, :] = wide_ref[H:].reshape(side, Z)
        sent[back][:side, :] = wide_ref[:H].reshape(side, Z)

    by_parity("gx", place)


def pack_next(v_ref, a_ref, b_ref, wide_ref, first_ref, second_ref):
    widen(v_ref, (a_ref, b_ref), wide_ref)
    sent = (first_ref, second_ref)
    side = H * GROUP

    def place(onward, back):
        sent[onward][...] = wide_ref[H:].reshape(side, Z)
        sent[back][...] = wide_ref[:H].reshape(side, Z)

    by_parity("gx", place)


def halves(v):
    high = v.astype(jnp.bfloat16)
    low = (v - high.astype(jnp.float32)).astype(jnp.bfloat16)
    return jnp.concatenate([high, low], axis=1)


def stationary(v):
    both = halves(v)
    return jnp.concatenate([both, both], axis=0)


def expanded(rows):
    fold = rows[34:40]
    source = (
        rows[:TAPS],
        rows[TAPS : 2 * TAPS],
        jnp.concatenate([fold, pltpu.roll(fold, 128 - FOLD, 1), pltpu.roll(fold, 128 - 2 * FOLD, 1)[:5]], axis=0),
    )
    lane = lax.broadcasted_iota(jnp.int32, (TAPS, 128), 1)
    tiles = []
    for u in range(5):
        tile = jnp.zeros((TAPS, 128), jnp.float32)
        for a in range(4 * u, min(4 * u + 4, TAPS)):
            begin, to = TAPS * a, GROUP * (a % 4)
            for k in sorted({begin // 128, (begin + TAPS - 1) // 128}):
                low, high = max(begin, 128 * k), min(begin + TAPS, 128 * (k + 1))
                shift = (to - begin) % 128
                moved = pltpu.roll(source[k], shift, 1) if shift else source[k]
                tile = jnp.where((lane >= to + low - begin) & (lane < to + high - begin), moved, tile)
        tiles.append(tile)
    return jnp.concatenate(tiles, axis=1)


def shifted(table, rows_ref, k):
    for r in range(4):
        rolled = table if r == 0 else pltpu.roll(table, GROUP * r, 1)
        for u in range(5):
            rows_ref[(k * 4 + r) * 5 + u, :TAPS, :] = rolled[:, u * 128 : (u + 1) * 128]


def own_rows(mine_ref, rows_ref):
    side = H * GROUP
    own, nexty = mine_ref[side : side + PACKED, :], mine_ref[side + PACKED :, :]
    for k, rows in enumerate((own, nexty - own)):
        shifted(expanded(rows), rows_ref, k)


def build(mine_ref, arrived, own_rows_ref, wa_ref, wb_ref, rows_ref, even_ref, odd_ref):
    side = H * GROUP
    own, nexty = mine_ref[side : side + PACKED, :], mine_ref[side + PACKED :, :]
    onward = jnp.where(even("gx"), arrived[0][side:, :], arrived[1][side:, :])
    nextx, corner = jnp.where(last("gx"), own, onward[:PACKED]), jnp.where(last("gx"), nexty, onward[PACKED:])
    across = nextx - own
    for k, rows in enumerate((across, corner - nexty - across)):
        shifted(expanded(0.25 * rows), rows_ref, 2 + k)
    for k in range(2):
        for r in range(4):
            for u in range(5):
                at = (k * 4 + r) * 5 + u
                rows_ref[at] = own_rows_ref[at] + ((r + 0.5) / 4) * rows_ref[at + 40]
    along = lax.broadcasted_iota(jnp.int32, (H, Z), 0).astype(jnp.float32)
    steps = [(along + (0.5 + H * half)) / T for half in range(2)]
    zero = jnp.zeros((T, 128), jnp.bfloat16)

    def spread(c, q_ref):
        for r in range(4):
            for u in range(5):
                for m in range(2):
                    at = (m * 8 + r) * 5 + u
                    near = rows_ref[at, pl.ds(c, H, stride=0), :]
                    step = rows_ref[at + 20, pl.ds(c, H, stride=0), :]
                    for half in range(2):
                        q_ref[m, r * 5 + u, half * H : (half + 1) * H, :] = pltpu.roll(
                            near + steps[half] * step, H * half, 1, stride=1, stride_axis=0
                        )

    def fill(c, q_ref):
        def base(x):
            return pl.multiple_of((((x // 8) * TAPS + c) * 8 + x % 8) * T, T)

        for r in range(4):
            for u in range(5):
                w, quarter = q_ref[0, r * 5 + u], q_ref[1, r * 5 + u]
                for q in range(4):
                    w = w if q == 0 else w + quarter
                    high = w.astype(jnp.bfloat16)
                    low = (w - high.astype(jnp.float32)).astype(jnp.bfloat16)
                    tile = q + u
                    rows = pl.ds(base(4 * q + r), T)
                    ref, at, width = (wa_ref, tile - 2, 4) if 2 <= tile < 6 else (wb_ref, tile % 2, 2)
                    ref[at, rows, :] = high
                    ref[at + width, rows, :] = low
            for q, ref, at, width in ((0, wa_ref, 3, 4), (1, wb_ref, 0, 2), (2, wb_ref, 1, 2), (3, wa_ref, 0, 4)):
                rows = pl.ds(base(4 * q + r), T)
                ref[at, rows, :] = zero
                ref[at + width, rows, :] = zero

    spread(0, even_ref)

    @pl.loop(0, TAPS // 2)
    def _(i):
        spread(2 * i + 1, odd_ref)
        fill(2 * i, even_ref)
        spread(2 * i + 2, even_ref)
        fill(2 * i + 1, odd_ref)

    fill(TAPS - 1, even_ref)


def joined(ref, rows):
    return jnp.concatenate([ref[t, rows, :] for t in range(ref.shape[0])], axis=1)


def product(w, v):
    both = jnp.dot(w, v, preferred_element_type=jnp.float32)
    return both[:, :Z] + both[:, Z:]


def inner_part(wide_ref, wa_ref, r_ref):
    v = stationary(wide_ref[...].reshape(T * GROUP, Z))
    for h in range(2):
        rows = slice(h * TAPS * 128, (h + 1) * TAPS * 128)
        r_ref[rows, :] = product(joined(wa_ref, rows), v)


def outer_part(arrived, wb_ref, r_ref, out_ref, side_ref):
    lane = lax.broadcasted_iota(jnp.int32, (128, Z), 1)

    def place(onward, back):
        side_ref[0] = arrived[back][: H * GROUP, :]
        side_ref[1] = arrived[onward][: H * GROUP, :]

    by_parity("gx", place)
    for h in range(2):
        v = stationary(side_ref[h])
        total = None
        for c in range(TAPS):
            at = slice((h * TAPS + c) * 128, (h * TAPS + c + 1) * 128)
            part = r_ref[at, :] + product(joined(wb_ref, at), v)
            if c != H:
                part = pltpu.roll(part, (H - c) % Z, 1)
                part = jnp.where((lane >= H - c) & (lane < Z + H - c), part, 0.0)
            total = part if total is None else total + part
        out_ref[h * 8 : (h + 1) * 8] = total.reshape(8, T, Z)


def step_one(d_ref, p_ref, wide_ref, mine_ref, a_ref, b_ref, own_rows_ref,
             wa_ref, wb_ref, model_ref, first_ref, second_ref, rows_ref, even_ref, odd_ref, r_ref, k_ref, side_ref):
    build(mine_ref, (a_ref, b_ref), own_rows_ref, wa_ref, wb_ref, rows_ref, even_ref, odd_ref)
    inner_part(wide_ref, wa_ref, r_ref)
    outer_part((a_ref, b_ref), wb_ref, r_ref, k_ref, side_ref)
    v = wide_ref[:, H : H + T, :]
    residual = d_ref[...] - (v + k_ref[...])
    model_ref[...] = v + relaxation * p_ref[...] * residual
    sent = (first_ref, second_ref)

    def place(onward, back):
        sent[onward][...] = model_ref[:, H:, :].reshape(T * H, Z)
        sent[back][...] = model_ref[:, :H, :].reshape(T * H, Z)

    by_parity("gy", place)


def step_two(d_ref, p_ref, v_ref, a_ref, b_ref, wb_ref, r_ref, model_ref, residual_ref, k_ref, side_ref):
    outer_part((a_ref, b_ref), wb_ref, r_ref, k_ref, side_ref)
    v = v_ref[...]
    residual = d_ref[...] - (v + k_ref[...])
    residual_ref[...] = residual
    model_ref[...] = v + relaxation * p_ref[...] * residual


def local(data, precond, psf):
    side = H * GROUP
    wide_shape = held(T, GROUP, Z)
    block = pltpu.VMEM((T, T, Z), jnp.float32)
    sides = pltpu.VMEM((2, side, Z), jnp.float32)
    row = held(T * H + PACKED, Z)
    tile = held(T, T, Z)
    psf = psf.reshape(DENSE, 1, TAPS)
    v, first, second, data, precond = call(
        prepare,
        (tile, row, row, tile, tile),
        4,
        [
            pltpu.VMEM((DENSE, 1, TAPS), jnp.float32),
            pltpu.VMEM((384, 128), jnp.float32),
            pltpu.SemaphoreType.DMA((3,)),
        ],
        pl.BlockSpec(memory_space=pltpu.HBM),
    )(*(pltpu.with_memory_space_constraint(x, pltpu.HBM) for x in (data, precond, psf)))
    a, b = swapped("gy", first, second)
    row = held(side + 2 * PACKED, Z)
    wide, first, second = call(pack_first, (wide_shape, row, row), 3)(*map(keep, (v, first, a, b)))
    a, b = swapped("gx", first, second)
    tables = call(own_rows, held(40, 24, 128), 2)(keep(first))
    row = held(T * H, Z)
    turned = pltpu.VMEM((2, 20, T, 128), jnp.float32)
    wa, wb, v, first, second = call(
        step_one,
        (held(8, ROWS, 128, dtype=jnp.bfloat16), held(4, ROWS, 128, dtype=jnp.bfloat16), held(T, T, Z), row, row),
        14,
        [pltpu.VMEM((80, 24, 128), jnp.float32), turned, turned, pltpu.VMEM((ROWS, Z), jnp.float32), block, sides],
    )(*map(keep, (data, precond, wide, first, a, b, tables)))
    a, b = swapped("gy", first, second)
    row = held(side, Z)
    wide, first, second = call(pack_next, (wide_shape, row, row), 3)(*map(keep, (v, a, b)))
    a, b = swapped("gx", first, second)
    part = call(inner_part, held(ROWS, Z), 8)(*map(keep, (wide, wa)))
    return call(step_two, (f32(T, T, Z), f32(T, T, Z)), 6, [block, sides])(
        *map(keep, (data, precond, v, a, b, wb, part))
    )


def solution(mesh):
    placed = (P("gx", "gy", None), P("gx", "gy", None), P("gx", "gy", None, None, None))
    return jax.shard_map(
        local,
        mesh=mesh,
        in_specs=placed,
        out_specs=(P("gx", "gy", None), P("gx", "gy", None)),
        check_vma=False,
    )
```

time: 65.8 us -> 60.8 us (0.924)
  local copies, waits for them, and re-layouts: 2.73 us -> 0 us
  waiting for transfers between devices: 21.9 us -> 19.2 us
    unnamed x5 -> x0, local copies, waits for them, and re-layouts: 2.73 us -> none
    ppermute x8, waiting for transfers between devices: 21.9 us -> 19.2 us  [swapped(): received.append(lax.ppermute(sent, axis, pairs))]
    pallas_call x6 -> x7, Pallas kernels: 13.4 us -> 13.5 us  [run(): pl.pallas_call(kernel, out_shape=outs, in_specs=[space] * len(operands),...]
  transfers between devices with their start and end apart: 8 -> 8, of which waited for: 4 -> 5; matrix products, arithmetic and copies ran while one was open for 0% -> 0% of each run, Pallas kernels for 4% -> 5%
where the time goes in v2:
time: 60.8 us; the launch traced here: 60.6 us
  starting transfers between devices  27.2 us (45%)
  waiting for transfers between devices  19.2 us (32%)
  Pallas kernels  13.5 us (22%)
  between operations  0.74 us (1%)
    ppermute x8, starting transfers between devices, swapped(): received.append(lax.ppermute(sent, axis, pairs))  27.2 us
    ppermute x8, waiting for transfers between devices, swapped(): received.append(lax.ppermute(sent, axis, pairs))  19.2 us
    pallas_call x7, Pallas kernels, run(): pl.pallas_call(kernel, out_shape=outs, in_specs=[space] * len(operands),...  13.5 us
  transfers between devices with their start and end apart: 8, of which 5 were waited for; matrix products, arithmetic and copies ran while one was open for 0% of the time, Pallas kernels for 5%

profile of v2, /device:TPU:57, one launch (start us, length us, event | category | flops | bytes accessed | tf_op | source)
XLA Modules:
  0.0 60.6 jit_solution(536731938584830179)
XLA Ops:
  0.6 1.2 %shard_map.50 = (f32[16,16,128]{2,1,0:T(8,128)S(1)}, f32[168,128]{1,0:T(8,128)S(1)}, f32[168,128]{1,0:T(8,128)S(1)}, f32[16,16,128]{2,1,0:T(8,128)S(1)}, f32[16,16,128]{2,1,0:T(8,128)S(1)}) custom-call(f32[16,16,128]{2,1,0:T(8,128)} %d_hbm.1, f32[16,16,128]{2,1,0:T(8,128)} %p_hbm.1, f32[289,1,17]{2,1,0:T(1,128)} %bitcast.1), custom_call_target="tpu_custom_call" | custom-call | tf_op jit(solution)/shard_map/pallas_call | solution.py:34
  1.8 6.1 %collective-permute-start = (f32[168,128]{1,0:T(8,128)S(1)}, f32[168,128]{1,0:T(8,128)S(1)}, u32[]{:S(2)}, u32[]{:S(2)}) collective-permute-start(f32[168,128]{1,0:T(8,128)S(1)} %get-tuple-element.21.own_ref), channel_id=1, source_target_pairs={{0,1},{1,0},{2,3},{3,2},{4,5},{5,4},{6,7},{7,6},{8,9},{9,8},{10,11... | collective-permute-start | bytes 258056 | tf_op jit(solution)/shard_map/ppermute | solution.py:61
  7.9 4.3 %collective-permute-start.1 = (f32[168,128]{1,0:T(8,128)S(1)}, f32[168,128]{1,0:T(8,128)S(1)}, u32[]{:S(2)}, u32[]{:S(2)}) collective-permute-start(f32[168,128]{1,0:T(8,128)S(1)} %get-tuple-element.22), channel_id=1, source_target_pairs={{1,2},{2,1},{3,4},{4,3},{5,6},{6,5},{7,8},{8,7},{9,10},{10,9},{11,... | collective-permute-start | bytes 258056 | tf_op jit(solution)/shard_map/ppermute | solution.py:61
  12.2 0.0 collective-permute-done.a_ref
  12.2 7.8 %collective-permute-done.1.b_ref = f32[168,128]{1,0:T(8,128)S(1)} collective-permute-done((f32[168,128]{1,0:T(8,128)S(1)}, f32[168,128]{1,0:T(8,128)S(1)}, u32[]{:S(2)}, u32[]{:S(2)}) %collective-permute-start.1) | collective-permute-done | bytes 86048 | tf_op jit(solution)/shard_map/ppermute | solution.py:61
  20.0 0.1 shard_map.51
  20.1 4.0 %collective-permute-start.2 = (f32[336,128]{1,0:T(8,128)S(1)}, f32[336,128]{1,0:T(8,128)S(1)}, u32[]{:S(2)}, u32[]{:S(2)}) collective-permute-start(f32[336,128]{1,0:T(8,128)S(1)} %get-tuple-element.24.mine_ref), channel_id=1, source_target_pairs={{0,32},{32,0},{64,96},{96,64},{128,160},{160,128},{192,224},{224,1... | collective-permute-start | bytes 516104 | tf_op jit(solution)/shard_map/ppermute | solution.py:61
  24.1 2.2 %collective-permute-start.3 = (f32[336,128]{1,0:T(8,128)S(1)}, f32[336,128]{1,0:T(8,128)S(1)}, u32[]{:S(2)}, u32[]{:S(2)}) collective-permute-start(f32[336,128]{1,0:T(8,128)S(1)} %get-tuple-element.25), channel_id=1, source_target_pairs={{32,64},{64,32},{96,128},{128,96},{160,192},{192,160},{33,65},{65,... | collective-permute-start | bytes 516104 | tf_op jit(solution)/shard_map/ppermute | solution.py:61
  26.3 0.4 shard_map.52.own_rows_ref
  26.7 0.0 collective-permute-done.2.a_ref
  26.7 4.1 %collective-permute-done.3.b_ref = f32[336,128]{1,0:T(8,128)S(1)} collective-permute-done((f32[336,128]{1,0:T(8,128)S(1)}, f32[336,128]{1,0:T(8,128)S(1)}, u32[]{:S(2)}, u32[]{:S(2)}) %collective-permute-start.3) | collective-permute-done | bytes 172064 | tf_op jit(solution)/shard_map/ppermute | solution.py:61
  30.8 7.1 %shard_map.53 = (bf16[8,4352,128]{2,1,0:T(8,128)(2,1)S(1)}, bf16[4,4352,128]{2,1,0:T(8,128)(2,1)S(1)}, f32[16,16,128]{2,1,0:T(8,128)S(1)}, f32[128,128]{1,0:T(8,128)S(1)}, f32[128,128]{1,0:T(8,128)S(1)}) custom-call(f32[16,16,128]{2,1,0:T(8,128)S(1)} %get-tuple-element.18.d_ref, f32[16,16,128]{2,1,0:T(8,128)S(1)} %get-tuple-element.19.p_ref, ...), custom_call_target="tpu_custom_call" | custom-call | tf_op jit(solution)/shard_map/pallas_call | solution.py:34
  37.9 0.1 collective-permute-start.4
  38.0 7.3 %collective-permute-start.5 = (f32[128,128]{1,0:T(8,128)S(1)}, f32[128,128]{1,0:T(8,128)S(1)}, u32[]{:S(2)}, u32[]{:S(2)}) collective-permute-start(f32[128,128]{1,0:T(8,128)S(1)} %get-tuple-element.28), channel_id=1, source_target_pairs={{1,2},{2,1},{3,4},{4,3},{5,6},{6,5},{7,8},{8,7},{9,10},{10,9},{11,... | collective-permute-start | bytes 196616 | tf_op jit(solution)/shard_map/ppermute | solution.py:61
  45.3 0.9 %collective-permute-done.4.a_ref = f32[128,128]{1,0:T(8,128)S(1)} collective-permute-done((f32[128,128]{1,0:T(8,128)S(1)}, f32[128,128]{1,0:T(8,128)S(1)}, u32[]{:S(2)}, u32[]{:S(2)}) %collective-permute-start.4) | collective-permute-done | bytes 65568 | tf_op jit(solution)/shard_map/ppermute | solution.py:61
  46.3 4.9 %collective-permute-done.5.b_ref = f32[128,128]{1,0:T(8,128)S(1)} collective-permute-done((f32[128,128]{1,0:T(8,128)S(1)}, f32[128,128]{1,0:T(8,128)S(1)}, u32[]{:S(2)}, u32[]{:S(2)}) %collective-permute-start.5) | collective-permute-done | bytes 65568 | tf_op jit(solution)/shard_map/ppermute | solution.py:61
  51.2 0.1 shard_map.54
  51.3 1.0 %collective-permute-start.6 = (f32[256,128]{1,0:T(8,128)S(1)}, f32[256,128]{1,0:T(8,128)S(1)}, u32[]{:S(2)}, u32[]{:S(2)}) collective-permute-start(f32[256,128]{1,0:T(8,128)S(1)} %get-tuple-element.29), channel_id=1, source_target_pairs={{0,32},{32,0},{64,96},{96,64},{128,160},{160,128},{192,224},{224,1... | collective-permute-start | bytes 393224 | tf_op jit(solution)/shard_map/ppermute | solution.py:61
  52.2 2.2 %collective-permute-start.7 = (f32[256,128]{1,0:T(8,128)S(1)}, f32[256,128]{1,0:T(8,128)S(1)}, u32[]{:S(2)}, u32[]{:S(2)}) collective-permute-start(f32[256,128]{1,0:T(8,128)S(1)} %get-tuple-element.30), channel_id=1, source_target_pairs={{32,64},{64,32},{96,128},{128,96},{160,192},{192,160},{33,65},{65,... | collective-permute-start | bytes 393224 | tf_op jit(solution)/shard_map/ppermute | solution.py:61
  54.5 2.6 %shard_map.55.r_ref = f32[4352,128]{1,0:T(8,128)S(1)} custom-call(f32[16,32,128]{2,1,0:T(8,128)S(1)} %get-tuple-element.32.wide_ref, bf16[8,4352,128]{2,1,0:T(8,128)(2,1)S(1)} %get-tuple-element.33.wa_ref), custom_call_target="tpu_custom_call" | custom-call | tf_op jit(solution)/shard_map/pallas_call | solution.py:34
  57.0 0.0 collective-permute-done.6.a_ref
  57.1 1.4 %collective-permute-done.7.b_ref = f32[256,128]{1,0:T(8,128)S(1)} collective-permute-done((f32[256,128]{1,0:T(8,128)S(1)}, f32[256,128]{1,0:T(8,128)S(1)}, u32[]{:S(2)}, u32[]{:S(2)}) %collective-permute-start.7) | collective-permute-done | bytes 131104 | tf_op jit(solution)/shard_map/ppermute | solution.py:61
  58.5 2.1 %shard_map.56 = (f32[16,16,128]{2,1,0:T(8,128)}, f32[16,16,128]{2,1,0:T(8,128)}) custom-call(f32[16,16,128]{2,1,0:T(8,128)S(1)} %get-tuple-element.18.d_ref, f32[16,16,128]{2,1,0:T(8,128)S(1)} %get-tuple-element.19.p_ref, f32[16,16,128]{2,1,0:T(8,128)S(1)} %get-tuple-element.26.v_ref, f32[256,128]{1,0:T(8,128)S(1)} %collective-permute-done.6.a_ref, ...), custom_call_target="tpu_custom_call" | custom-call | tf_op jit(solution)/shard_map/pallas_call | solution.py:34
Async XLA Ops:
  1.8 10.4 %collective-permute-start = (f32[168,128]{1,0:T(8,128)S(1)}, f32[168,128]{1,0:T(8,128)S(1)}, u32[]{:S(2)}, u32[]{:S(2)}) collective-permute-start(f32[168,128]{1,0:T(8,128)S(1)} %get-tuple-element.21.own_ref), channel_id=1, source_target_pairs={{0,1},{1,0},{2,3},{3,2},{4,5},{5,4},{6,7},{7,6},{8,9},{9,8},{10,11... | collective-permute-start | bytes 258056 | tf_op jit(solution)/shard_map/ppermute | solution.py:61
  7.9 12.1 %collective-permute-start.1 = (f32[168,128]{1,0:T(8,128)S(1)}, f32[168,128]{1,0:T(8,128)S(1)}, u32[]{:S(2)}, u32[]{:S(2)}) collective-permute-start(f32[168,128]{1,0:T(8,128)S(1)} %get-tuple-element.22), channel_id=1, source_target_pairs={{1,2},{2,1},{3,4},{4,3},{5,6},{6,5},{7,8},{8,7},{9,10},{10,9},{11,... | collective-permute-start | bytes 258056 | tf_op jit(solution)/shard_map/ppermute | solution.py:61
  20.1 6.6 %collective-permute-start.2 = (f32[336,128]{1,0:T(8,128)S(1)}, f32[336,128]{1,0:T(8,128)S(1)}, u32[]{:S(2)}, u32[]{:S(2)}) collective-permute-start(f32[336,128]{1,0:T(8,128)S(1)} %get-tuple-element.24.mine_ref), channel_id=1, source_target_pairs={{0,32},{32,0},{64,96},{96,64},{128,160},{160,128},{192,224},{224,1... | collective-permute-start | bytes 516104 | tf_op jit(solution)/shard_map/ppermute | solution.py:61
  24.1 6.7 %collective-permute-start.3 = (f32[336,128]{1,0:T(8,128)S(1)}, f32[336,128]{1,0:T(8,128)S(1)}, u32[]{:S(2)}, u32[]{:S(2)}) collective-permute-start(f32[336,128]{1,0:T(8,128)S(1)} %get-tuple-element.25), channel_id=1, source_target_pairs={{32,64},{64,32},{96,128},{128,96},{160,192},{192,160},{33,65},{65,... | collective-permute-start | bytes 516104 | tf_op jit(solution)/shard_map/ppermute | solution.py:61
  37.9 8.3 %collective-permute-start.4 = (f32[128,128]{1,0:T(8,128)S(1)}, f32[128,128]{1,0:T(8,128)S(1)}, u32[]{:S(2)}, u32[]{:S(2)}) collective-permute-start(f32[128,128]{1,0:T(8,128)S(1)} %get-tuple-element.27), channel_id=1, source_target_pairs={{0,1},{1,0},{2,3},{3,2},{4,5},{5,4},{6,7},{7,6},{8,9},{9,8},{10,11... | collective-permute-start | bytes 196616 | tf_op jit(solution)/shard_map/ppermute | solution.py:61
  38.0 13.2 %collective-permute-start.5 = (f32[128,128]{1,0:T(8,128)S(1)}, f32[128,128]{1,0:T(8,128)S(1)}, u32[]{:S(2)}, u32[]{:S(2)}) collective-permute-start(f32[128,128]{1,0:T(8,128)S(1)} %get-tuple-element.28), channel_id=1, source_target_pairs={{1,2},{2,1},{3,4},{4,3},{5,6},{6,5},{7,8},{8,7},{9,10},{10,9},{11,... | collective-permute-start | bytes 196616 | tf_op jit(solution)/shard_map/ppermute | solution.py:61
  51.3 5.8 %collective-permute-start.6 = (f32[256,128]{1,0:T(8,128)S(1)}, f32[256,128]{1,0:T(8,128)S(1)}, u32[]{:S(2)}, u32[]{:S(2)}) collective-permute-start(f32[256,128]{1,0:T(8,128)S(1)} %get-tuple-element.29), channel_id=1, source_target_pairs={{0,32},{32,0},{64,96},{96,64},{128,160},{160,128},{192,224},{224,1... | collective-permute-start | bytes 393224 | tf_op jit(solution)/shard_map/ppermute | solution.py:61
  52.2 6.3 %collective-permute-start.7 = (f32[256,128]{1,0:T(8,128)S(1)}, f32[256,128]{1,0:T(8,128)S(1)}, u32[]{:S(2)}, u32[]{:S(2)}) collective-permute-start(f32[256,128]{1,0:T(8,128)S(1)} %get-tuple-element.30), channel_id=1, source_target_pairs={{32,64},{64,32},{96,128},{128,96},{160,192},{192,160},{33,65},{65,... | collective-permute-start | bytes 393224 | tf_op jit(solution)/shard_map/ppermute | solution.py:61

commit v3 on v2

--- a/solution.py
+++ b/solution.py
@@ -190,7 +190,7 @@
         shifted(expanded(rows), rows_ref, k)
 
 
-def build(mine_ref, arrived, own_rows_ref, wa_ref, wb_ref, rows_ref, even_ref, odd_ref):
+def build(mine_ref, arrived, own_rows_ref, wa_ref, wb_ref, rows_ref, even_ref, odd_ref, use):
     side = H * GROUP
     own, nexty = mine_ref[side : side + PACKED, :], mine_ref[side + PACKED :, :]
     onward = jnp.where(even("gx"), arrived[0][side:, :], arrived[1][side:, :])
@@ -221,7 +221,7 @@
 
     def fill(c, q_ref):
         def base(x):
-            return pl.multiple_of((((x // 8) * TAPS + c) * 8 + x % 8) * T, T)
+            return (((x // 8) * TAPS + c) * 8 + x % 8) * T
 
         for r in range(4):
             for u in range(5):
@@ -240,16 +240,16 @@
                 ref[at, rows, :] = zero
                 ref[at + width, rows, :] = zero
 
+    held_refs = (even_ref, odd_ref)
     spread(0, even_ref)
-
-    @pl.loop(0, TAPS // 2)
-    def _(i):
-        spread(2 * i + 1, odd_ref)
-        fill(2 * i, even_ref)
-        spread(2 * i + 2, even_ref)
-        fill(2 * i + 1, odd_ref)
-
-    fill(TAPS - 1, even_ref)
+    spread(1, odd_ref)
+    fill(0, even_ref)
+    for c in range(TAPS):
+        use(c)
+        if c + 1 < TAPS:
+            fill(c + 1, held_refs[(c + 1) % 2])
+        if c + 2 < TAPS:
+            spread(c + 2, held_refs[c % 2])
 
 
 def joined(ref, rows):
@@ -268,34 +268,51 @@
         r_ref[rows, :] = product(joined(wa_ref, rows), v)
 
 
-def outer_part(arrived, wb_ref, r_ref, out_ref, side_ref):
-    lane = lax.broadcasted_iota(jnp.int32, (128, Z), 1)
-
+def moved(part, c):
+    if c == H:
+        return part
+    lane = lax.broadcasted_iota(jnp.int32, part.shape, 1)
+    return jnp.where((lane >= H - c) & (lane < Z + H - c), pltpu.roll(part, (H - c) % Z, 1), 0.0)
+
+
+def sides(arrived, side_ref):
     def place(onward, back):
         side_ref[0] = arrived[back][: H * GROUP, :]
         side_ref[1] = arrived[onward][: H * GROUP, :]
 
     by_parity("gx", place)
+
+
+def outer_part(arrived, wb_ref, r_ref, out_ref, side_ref):
+    sides(arrived, side_ref)
     for h in range(2):
         v = stationary(side_ref[h])
         total = None
         for c in range(TAPS):
             at = slice((h * TAPS + c) * 128, (h * TAPS + c + 1) * 128)
-            part = r_ref[at, :] + product(joined(wb_ref, at), v)
-            if c != H:
-                part = pltpu.roll(part, (H - c) % Z, 1)
-                part = jnp.where((lane >= H - c) & (lane < Z + H - c), part, 0.0)
+            part = moved(r_ref[at, :] + product(joined(wb_ref, at), v), c)
             total = part if total is None else total + part
         out_ref[h * 8 : (h + 1) * 8] = total.reshape(8, T, Z)
 
 
 def step_one(d_ref, p_ref, wide_ref, mine_ref, a_ref, b_ref, own_rows_ref,
-             wa_ref, wb_ref, model_ref, first_ref, second_ref, rows_ref, even_ref, odd_ref, r_ref, k_ref, side_ref):
-    build(mine_ref, (a_ref, b_ref), own_rows_ref, wa_ref, wb_ref, rows_ref, even_ref, odd_ref)
-    inner_part(wide_ref, wa_ref, r_ref)
-    outer_part((a_ref, b_ref), wb_ref, r_ref, k_ref, side_ref)
+             wa_ref, wb_ref, model_ref, first_ref, second_ref, rows_ref, even_ref, odd_ref, all_ref, k_ref, side_ref):
+    sides((a_ref, b_ref), side_ref)
+    inner = stationary(wide_ref[...].reshape(T * GROUP, Z))
+    for h in range(2):
+        all_ref[h, : 4 * 256, :] = inner
+        all_ref[h, 4 * 256 :, :] = stationary(side_ref[h])
+
+    def use(c):
+        for h in range(2):
+            at = slice((h * TAPS + c) * 128, (h * TAPS + c + 1) * 128)
+            w = jnp.concatenate([joined(wa_ref, at), joined(wb_ref, at)], axis=1)
+            part = moved(product(w, all_ref[h]), c)
+            k_ref[h] = part if c == 0 else k_ref[h] + part
+
+    build(mine_ref, (a_ref, b_ref), own_rows_ref, wa_ref, wb_ref, rows_ref, even_ref, odd_ref, use)
     v = wide_ref[:, H : H + T, :]
-    residual = d_ref[...] - (v + k_ref[...])
+    residual = d_ref[...] - (v + k_ref[...].reshape(T, T, Z))
     model_ref[...] = v + relaxation * p_ref[...] * residual
     sent = (first_ref, second_ref)
 
@@ -318,7 +335,7 @@
     side = H * GROUP
     wide_shape = held(T, GROUP, Z)
     block = pltpu.VMEM((T, T, Z), jnp.float32)
-    sides = pltpu.VMEM((2, side, Z), jnp.float32)
+    edges = pltpu.VMEM((2, side, Z), jnp.float32)
     row = held(T * H + PACKED, Z)
     tile = held(T, T, Z)
     psf = psf.reshape(DENSE, 1, TAPS)
@@ -344,14 +361,21 @@
         step_one,
         (held(8, ROWS, 128, dtype=jnp.bfloat16), held(4, ROWS, 128, dtype=jnp.bfloat16), held(T, T, Z), row, row),
         14,
-        [pltpu.VMEM((80, 24, 128), jnp.float32), turned, turned, pltpu.VMEM((ROWS, Z), jnp.float32), block, sides],
+        [
+            pltpu.VMEM((80, 24, 128), jnp.float32),
+            turned,
+            turned,
+            pltpu.VMEM((2, 6 * 256, 2 * Z), jnp.bfloat16),
+            pltpu.VMEM((2, 128, Z), jnp.float32),
+            edges,
+        ],
     )(*map(keep, (data, precond, wide, first, a, b, tables)))
     a, b = swapped("gy", first, second)
     row = held(side, Z)
     wide, first, second = call(pack_next, (wide_shape, row, row), 3)(*map(keep, (v, a, b)))
     a, b = swapped("gx", first, second)
     part = call(inner_part, held(ROWS, Z), 8)(*map(keep, (wide, wa)))
-    return call(step_two, (f32(T, T, Z), f32(T, T, Z)), 6, [block, sides])(
+    return call(step_two, (f32(T, T, Z), f32(T, T, Z)), 6, [block, edges])(
         *map(keep, (data, precond, v, a, b, wb, part))
     )
 

time: 60.8 us -> 58.8 us (0.967)
  Pallas kernels: 13.5 us -> 11.4 us
    pallas_call x7, Pallas kernels: 13.5 us -> 11.4 us  [run(): pl.pallas_call(kernel, out_shape=outs, in_specs=[space] * len(operands),...]
where the time goes in v3:
time: 58.8 us; the launch traced here: 58.6 us
  starting transfers between devices  27.2 us (46%)
  waiting for transfers between devices  19.2 us (33%)
  Pallas kernels  11.4 us (19%)
  between operations  0.74 us (1%)
    ppermute x8, starting transfers between devices, swapped(): received.append(lax.ppermute(sent, axis, pairs))  27.2 us
    ppermute x8, waiting for transfers between devices, swapped(): received.append(lax.ppermute(sent, axis, pairs))  19.2 us
    pallas_call x7, Pallas kernels, run(): pl.pallas_call(kernel, out_shape=outs, in_specs=[space] * len(operands),...  11.4 us
  transfers between devices with their start and end apart: 8, of which 5 were waited for; matrix products, arithmetic and copies ran while one was open for 0% of the time, Pallas kernels for 5%

profile of v3, /device:TPU:57, one launch (start us, length us, event | category | flops | bytes accessed | tf_op | source)
XLA Modules:
  0.0 58.6 jit_solution(14948711935079846455)
XLA Ops:
  0.6 1.2 %shard_map.50 = (f32[16,16,128]{2,1,0:T(8,128)S(1)}, f32[168,128]{1,0:T(8,128)S(1)}, f32[168,128]{1,0:T(8,128)S(1)}, f32[16,16,128]{2,1,0:T(8,128)S(1)}, f32[16,16,128]{2,1,0:T(8,128)S(1)}) custom-call(f32[16,16,128]{2,1,0:T(8,128)} %d_hbm.1, f32[16,16,128]{2,1,0:T(8,128)} %p_hbm.1, f32[289,1,17]{2,1,0:T(1,128)} %bitcast.1), custom_call_target="tpu_custom_call" | custom-call | tf_op jit(solution)/shard_map/pallas_call | solution.py:34
  1.8 6.1 %collective-permute-start = (f32[168,128]{1,0:T(8,128)S(1)}, f32[168,128]{1,0:T(8,128)S(1)}, u32[]{:S(2)}, u32[]{:S(2)}) collective-permute-start(f32[168,128]{1,0:T(8,128)S(1)} %get-tuple-element.21.own_ref), channel_id=1, source_target_pairs={{0,1},{1,0},{2,3},{3,2},{4,5},{5,4},{6,7},{7,6},{8,9},{9,8},{10,11... | collective-permute-start | bytes 258056 | tf_op jit(solution)/shard_map/ppermute | solution.py:61
  7.9 4.3 %collective-permute-start.1 = (f32[168,128]{1,0:T(8,128)S(1)}, f32[168,128]{1,0:T(8,128)S(1)}, u32[]{:S(2)}, u32[]{:S(2)}) collective-permute-start(f32[168,128]{1,0:T(8,128)S(1)} %get-tuple-element.22), channel_id=1, source_target_pairs={{1,2},{2,1},{3,4},{4,3},{5,6},{6,5},{7,8},{8,7},{9,10},{10,9},{11,... | collective-permute-start | bytes 258056 | tf_op jit(solution)/shard_map/ppermute | solution.py:61
  12.2 0.0 collective-permute-done.a_ref
  12.2 7.8 %collective-permute-done.1.b_ref = f32[168,128]{1,0:T(8,128)S(1)} collective-permute-done((f32[168,128]{1,0:T(8,128)S(1)}, f32[168,128]{1,0:T(8,128)S(1)}, u32[]{:S(2)}, u32[]{:S(2)}) %collective-permute-start.1) | collective-permute-done | bytes 86048 | tf_op jit(solution)/shard_map/ppermute | solution.py:61
  20.0 0.1 shard_map.51
  20.1 4.0 %collective-permute-start.2 = (f32[336,128]{1,0:T(8,128)S(1)}, f32[336,128]{1,0:T(8,128)S(1)}, u32[]{:S(2)}, u32[]{:S(2)}) collective-permute-start(f32[336,128]{1,0:T(8,128)S(1)} %get-tuple-element.24.mine_ref), channel_id=1, source_target_pairs={{0,32},{32,0},{64,96},{96,64},{128,160},{160,128},{192,224},{224,1... | collective-permute-start | bytes 516104 | tf_op jit(solution)/shard_map/ppermute | solution.py:61
  24.1 2.2 %collective-permute-start.3 = (f32[336,128]{1,0:T(8,128)S(1)}, f32[336,128]{1,0:T(8,128)S(1)}, u32[]{:S(2)}, u32[]{:S(2)}) collective-permute-start(f32[336,128]{1,0:T(8,128)S(1)} %get-tuple-element.25), channel_id=1, source_target_pairs={{32,64},{64,32},{96,128},{128,96},{160,192},{192,160},{33,65},{65,... | collective-permute-start | bytes 516104 | tf_op jit(solution)/shard_map/ppermute | solution.py:61
  26.3 0.4 shard_map.52.own_rows_ref
  26.7 0.0 collective-permute-done.2.a_ref
  26.7 4.1 %collective-permute-done.3.b_ref = f32[336,128]{1,0:T(8,128)S(1)} collective-permute-done((f32[336,128]{1,0:T(8,128)S(1)}, f32[336,128]{1,0:T(8,128)S(1)}, u32[]{:S(2)}, u32[]{:S(2)}) %collective-permute-start.3) | collective-permute-done | bytes 172064 | tf_op jit(solution)/shard_map/ppermute | solution.py:61
  30.8 5.1 %shard_map.53 = (bf16[8,4352,128]{2,1,0:T(8,128)(2,1)S(1)}, bf16[4,4352,128]{2,1,0:T(8,128)(2,1)S(1)}, f32[16,16,128]{2,1,0:T(8,128)S(1)}, f32[128,128]{1,0:T(8,128)S(1)}, f32[128,128]{1,0:T(8,128)S(1)}) custom-call(f32[16,16,128]{2,1,0:T(8,128)S(1)} %get-tuple-element.18.d_ref, f32[16,16,128]{2,1,0:T(8,128)S(1)} %get-tuple-element.19.p_ref, ...), custom_call_target="tpu_custom_call" | custom-call | tf_op jit(solution)/shard_map/pallas_call | solution.py:34
  35.9 0.1 collective-permute-start.4
  36.0 7.3 %collective-permute-start.5 = (f32[128,128]{1,0:T(8,128)S(1)}, f32[128,128]{1,0:T(8,128)S(1)}, u32[]{:S(2)}, u32[]{:S(2)}) collective-permute-start(f32[128,128]{1,0:T(8,128)S(1)} %get-tuple-element.28), channel_id=1, source_target_pairs={{1,2},{2,1},{3,4},{4,3},{5,6},{6,5},{7,8},{8,7},{9,10},{10,9},{11,... | collective-permute-start | bytes 196616 | tf_op jit(solution)/shard_map/ppermute | solution.py:61
  43.2 0.9 %collective-permute-done.4.a_ref = f32[128,128]{1,0:T(8,128)S(1)} collective-permute-done((f32[128,128]{1,0:T(8,128)S(1)}, f32[128,128]{1,0:T(8,128)S(1)}, u32[]{:S(2)}, u32[]{:S(2)}) %collective-permute-start.4) | collective-permute-done | bytes 65568 | tf_op jit(solution)/shard_map/ppermute | solution.py:61
  44.2 4.9 %collective-permute-done.5.b_ref = f32[128,128]{1,0:T(8,128)S(1)} collective-permute-done((f32[128,128]{1,0:T(8,128)S(1)}, f32[128,128]{1,0:T(8,128)S(1)}, u32[]{:S(2)}, u32[]{:S(2)}) %collective-permute-start.5) | collective-permute-done | bytes 65568 | tf_op jit(solution)/shard_map/ppermute | solution.py:61
  49.1 0.1 shard_map.54
  49.2 1.0 %collective-permute-start.6 = (f32[256,128]{1,0:T(8,128)S(1)}, f32[256,128]{1,0:T(8,128)S(1)}, u32[]{:S(2)}, u32[]{:S(2)}) collective-permute-start(f32[256,128]{1,0:T(8,128)S(1)} %get-tuple-element.29), channel_id=1, source_target_pairs={{0,32},{32,0},{64,96},{96,64},{128,160},{160,128},{192,224},{224,1... | collective-permute-start | bytes 393224 | tf_op jit(solution)/shard_map/ppermute | solution.py:61
  50.1 2.2 %collective-permute-start.7 = (f32[256,128]{1,0:T(8,128)S(1)}, f32[256,128]{1,0:T(8,128)S(1)}, u32[]{:S(2)}, u32[]{:S(2)}) collective-permute-start(f32[256,128]{1,0:T(8,128)S(1)} %get-tuple-element.30), channel_id=1, source_target_pairs={{32,64},{64,32},{96,128},{128,96},{160,192},{192,160},{33,65},{65,... | collective-permute-start | bytes 393224 | tf_op jit(solution)/shard_map/ppermute | solution.py:61
  52.4 2.6 %shard_map.55.r_ref = f32[4352,128]{1,0:T(8,128)S(1)} custom-call(f32[16,32,128]{2,1,0:T(8,128)S(1)} %get-tuple-element.32.wide_ref, bf16[8,4352,128]{2,1,0:T(8,128)(2,1)S(1)} %get-tuple-element.33.wa_ref), custom_call_target="tpu_custom_call" | custom-call | tf_op jit(solution)/shard_map/pallas_call | solution.py:34
  55.0 0.0 collective-permute-done.6.a_ref
  55.0 1.4 %collective-permute-done.7.b_ref = f32[256,128]{1,0:T(8,128)S(1)} collective-permute-done((f32[256,128]{1,0:T(8,128)S(1)}, f32[256,128]{1,0:T(8,128)S(1)}, u32[]{:S(2)}, u32[]{:S(2)}) %collective-permute-start.7) | collective-permute-done | bytes 131104 | tf_op jit(solution)/shard_map/ppermute | solution.py:61
  56.4 2.1 %shard_map.56 = (f32[16,16,128]{2,1,0:T(8,128)}, f32[16,16,128]{2,1,0:T(8,128)}) custom-call(f32[16,16,128]{2,1,0:T(8,128)S(1)} %get-tuple-element.18.d_ref, f32[16,16,128]{2,1,0:T(8,128)S(1)} %get-tuple-element.19.p_ref, f32[16,16,128]{2,1,0:T(8,128)S(1)} %get-tuple-element.26.v_ref, f32[256,128]{1,0:T(8,128)S(1)} %collective-permute-done.6.a_ref, ...), custom_call_target="tpu_custom_call" | custom-call | tf_op jit(solution)/shard_map/pallas_call | solution.py:34
Async XLA Ops:
  1.8 10.4 %collective-permute-start = (f32[168,128]{1,0:T(8,128)S(1)}, f32[168,128]{1,0:T(8,128)S(1)}, u32[]{:S(2)}, u32[]{:S(2)}) collective-permute-start(f32[168,128]{1,0:T(8,128)S(1)} %get-tuple-element.21.own_ref), channel_id=1, source_target_pairs={{0,1},{1,0},{2,3},{3,2},{4,5},{5,4},{6,7},{7,6},{8,9},{9,8},{10,11... | collective-permute-start | bytes 258056 | tf_op jit(solution)/shard_map/ppermute | solution.py:61
  7.9 12.1 %collective-permute-start.1 = (f32[168,128]{1,0:T(8,128)S(1)}, f32[168,128]{1,0:T(8,128)S(1)}, u32[]{:S(2)}, u32[]{:S(2)}) collective-permute-start(f32[168,128]{1,0:T(8,128)S(1)} %get-tuple-element.22), channel_id=1, source_target_pairs={{1,2},{2,1},{3,4},{4,3},{5,6},{6,5},{7,8},{8,7},{9,10},{10,9},{11,... | collective-permute-start | bytes 258056 | tf_op jit(solution)/shard_map/ppermute | solution.py:61
  20.1 6.6 %collective-permute-start.2 = (f32[336,128]{1,0:T(8,128)S(1)}, f32[336,128]{1,0:T(8,128)S(1)}, u32[]{:S(2)}, u32[]{:S(2)}) collective-permute-start(f32[336,128]{1,0:T(8,128)S(1)} %get-tuple-element.24.mine_ref), channel_id=1, source_target_pairs={{0,32},{32,0},{64,96},{96,64},{128,160},{160,128},{192,224},{224,1... | collective-permute-start | bytes 516104 | tf_op jit(solution)/shard_map/ppermute | solution.py:61
  24.1 6.7 %collective-permute-start.3 = (f32[336,128]{1,0:T(8,128)S(1)}, f32[336,128]{1,0:T(8,128)S(1)}, u32[]{:S(2)}, u32[]{:S(2)}) collective-permute-start(f32[336,128]{1,0:T(8,128)S(1)} %get-tuple-element.25), channel_id=1, source_target_pairs={{32,64},{64,32},{96,128},{128,96},{160,192},{192,160},{33,65},{65,... | collective-permute-start | bytes 516104 | tf_op jit(solution)/shard_map/ppermute | solution.py:61
  35.9 8.3 %collective-permute-start.4 = (f32[128,128]{1,0:T(8,128)S(1)}, f32[128,128]{1,0:T(8,128)S(1)}, u32[]{:S(2)}, u32[]{:S(2)}) collective-permute-start(f32[128,128]{1,0:T(8,128)S(1)} %get-tuple-element.27), channel_id=1, source_target_pairs={{0,1},{1,0},{2,3},{3,2},{4,5},{5,4},{6,7},{7,6},{8,9},{9,8},{10,11... | collective-permute-start | bytes 196616 | tf_op jit(solution)/shard_map/ppermute | solution.py:61
  36.0 13.1 %collective-permute-start.5 = (f32[128,128]{1,0:T(8,128)S(1)}, f32[128,128]{1,0:T(8,128)S(1)}, u32[]{:S(2)}, u32[]{:S(2)}) collective-permute-start(f32[128,128]{1,0:T(8,128)S(1)} %get-tuple-element.28), channel_id=1, source_target_pairs={{1,2},{2,1},{3,4},{4,3},{5,6},{6,5},{7,8},{8,7},{9,10},{10,9},{11,... | collective-permute-start | bytes 196616 | tf_op jit(solution)/shard_map/ppermute | solution.py:61
  49.2 5.8 %collective-permute-start.6 = (f32[256,128]{1,0:T(8,128)S(1)}, f32[256,128]{1,0:T(8,128)S(1)}, u32[]{:S(2)}, u32[]{:S(2)}) collective-permute-start(f32[256,128]{1,0:T(8,128)S(1)} %get-tuple-element.29), channel_id=1, source_target_pairs={{0,32},{32,0},{64,96},{96,64},{128,160},{160,128},{192,224},{224,1... | collective-permute-start | bytes 393224 | tf_op jit(solution)/shard_map/ppermute | solution.py:61
  50.1 6.3 %collective-permute-start.7 = (f32[256,128]{1,0:T(8,128)S(1)}, f32[256,128]{1,0:T(8,128)S(1)}, u32[]{:S(2)}, u32[]{:S(2)}) collective-permute-start(f32[256,128]{1,0:T(8,128)S(1)} %get-tuple-element.30), channel_id=1, source_target_pairs={{32,64},{64,32},{96,128},{128,96},{160,192},{192,160},{33,65},{65,... | collective-permute-start | bytes 393224 | tf_op jit(solution)/shard_map/ppermute | solution.py:61

commit v4 on v3

v4 whole, which is shorter than its diff:
```python
import jax
import jax.numpy as jnp
from jax import lax
from jax.experimental import pallas as pl
from jax.experimental.pallas import tpu as pltpu
from jax.sharding import PartitionSpec as P


relaxation = 0.7

H = 8
TAPS = 17
T = 16
Z = 128
GROUP = 32
DENSE = TAPS * TAPS
ROWS = 2 * TAPS * 8 * T
PACKED = 40
FOLD = 40
VMEM = pl.BlockSpec(memory_space=pltpu.VMEM)
MIB = 1 << 20


def held(*shape, dtype=jnp.float32):
    return pltpu.VMEM(shape, dtype)


def keep(x):
    return pltpu.with_memory_space_constraint(x, pltpu.VMEM)


def call(kernel, outs, mib, scratch=(), space=VMEM, alias={}):
    def run(*operands):
        return pl.pallas_call(
            kernel,
            out_shape=outs,
            in_specs=[space] * len(operands),
            out_specs=jax.tree.map(lambda _: VMEM, outs),
            scratch_shapes=list(scratch),
            input_output_aliases=alias,
            compiler_params=pltpu.CompilerParams(vmem_limit_bytes=int(mib * MIB)),
        )(*operands)

    return run


def even(axis):
    return lax.axis_index(axis) % 2 == 0


def last(axis):
    return lax.axis_index(axis) == lax.axis_size(axis) - 1


def swapped(axis, first, second):
    size = lax.axis_size(axis)
    received = []
    for start, sent in ((0, first), (1, second)):
        pairs = []
        for i in range(start, size - 1, 2):
            pairs += [(i, i + 1), (i + 1, i)]
        received.append(lax.ppermute(sent, axis, pairs))
    return received


def by_parity(axis, action):
    pl.when(even(axis))(lambda: action(0, 1))
    pl.when(jnp.logical_not(even(axis)))(lambda: action(1, 0))


def f32(*shape):
    return jax.ShapeDtypeStruct(shape, jnp.float32)


def columns(v_ref, sent):
    def place(onward, back):
        sent[onward][: T * H, :] = v_ref[:, H:, :].reshape(T * H, Z)
        sent[back][: T * H, :] = v_ref[:, :H, :].reshape(T * H, Z)

    by_parity("gy", place)


def rows(v_ref, sent):
    def place(onward, back):
        sent[onward][: T * H, :] = v_ref[H:].reshape(T * H, Z)
        sent[back][: T * H, :] = v_ref[:H].reshape(T * H, Z)

    by_parity("gx", place)


def corners(wide_ref, sent):
    def place(onward, back):
        for ref, half in ((sent[onward], wide_ref.at[H:]), (sent[back], wide_ref.at[:H])):
            ref[: T * H, :] = jnp.concatenate([half[:, :H, :], half[:, H + T :, :]], axis=1).reshape(T * H, Z)

    by_parity("gx", place)


def prepare(d_hbm, p_hbm, psf_hbm, v_ref, first_ref, second_ref, xfirst_ref, xsecond_ref, d_ref, p_ref, psf_ref, t_ref, sems):
    copies = [
        pltpu.make_async_copy(src, dst, sems.at[k])
        for k, (src, dst) in enumerate(((psf_hbm, psf_ref.at[:DENSE]), (d_hbm, d_ref), (p_hbm, p_ref)))
    ]
    for copy in copies:
        copy.start()
    t_ref[DENSE:, :] = jnp.zeros((384 - DENSE, 128), jnp.float32)
    copies[0].wait()
    t_ref[:DENSE, :TAPS] = psf_ref[:DENSE, 0, :]
    turned = t_ref[...].T
    sent = (first_ref, second_ref)
    rest = turned[:TAPS, 256:]
    rest = jnp.where(lax.broadcasted_iota(jnp.int32, rest.shape, 1) < DENSE - 256, rest, 0.0)
    for ref in sent + (xfirst_ref, xsecond_ref):
        at = T * H
        ref[at : at + TAPS, :] = turned[:TAPS, :128]
        ref[at + TAPS : at + 2 * TAPS, :] = turned[:TAPS, 128:256]
        ref[at + 34 : at + 40, :] = rest[:6] + pltpu.roll(rest, FOLD, 1)[6:12]
        ref[at + 34 : at + 39, :] += pltpu.roll(rest, 2 * FOLD, 1)[12:17]
    copies[1].wait()
    copies[2].wait()
    v_ref[...] = d_ref[...] * p_ref[...]

    columns(v_ref, sent)
    rows(v_ref, (xfirst_ref, xsecond_ref))


def widen(v_ref, arrived, wide_ref):
    wide_ref[:, H : H + T, :] = v_ref[...]

    def place(onward, back):
        wide_ref[:, :H, :] = arrived[back][: T * H, :].reshape(T, H, Z)
        wide_ref[:, H + T :, :] = arrived[onward][: T * H, :].reshape(T, H, Z)

    by_parity("gy", place)


def pack_first(v_ref, own_ref, a_ref, b_ref, wide_ref, first_ref, second_ref):
    widen(v_ref, (a_ref, b_ref), wide_ref)

    def kernels(onward, back):
        for ref in (first_ref, second_ref):
            ref[T * H :, :] = jnp.where(last("gy"), own_ref[T * H :, :], (a_ref, b_ref)[onward][T * H :, :])

    by_parity("gy", kernels)
    corners(wide_ref, (first_ref, second_ref))


def pack_next(v_ref, a_ref, b_ref, wide_ref, first_ref, second_ref):
    widen(v_ref, (a_ref, b_ref), wide_ref)
    sent = (first_ref, second_ref)

    def place(onward, back):
        sent[onward][...] = wide_ref[H:]
        sent[back][...] = wide_ref[:H]

    by_parity("gx", place)


def halves(v):
    high = v.astype(jnp.bfloat16)
    low = (v - high.astype(jnp.float32)).astype(jnp.bfloat16)
    return jnp.concatenate([high, low], axis=1)


def stationary(v):
    both = halves(v)
    return jnp.concatenate([both, both], axis=0)


def expanded(rows):
    fold = rows[34:40]
    source = (
        rows[:TAPS],
        rows[TAPS : 2 * TAPS],
        jnp.concatenate([fold, pltpu.roll(fold, 128 - FOLD, 1), pltpu.roll(fold, 128 - 2 * FOLD, 1)[:5]], axis=0),
    )
    lane = lax.broadcasted_iota(jnp.int32, (TAPS, 128), 1)
    tiles = []
    for u in range(5):
        tile = jnp.zeros((TAPS, 128), jnp.float32)
        for a in range(4 * u, min(4 * u + 4, TAPS)):
            begin, to = TAPS * a, GROUP * (a % 4)
            for k in sorted({begin // 128, (begin + TAPS - 1) // 128}):
                low, high = max(begin, 128 * k), min(begin + TAPS, 128 * (k + 1))
                shift = (to - begin) % 128
                moved = pltpu.roll(source[k], shift, 1) if shift else source[k]
                tile = jnp.where((lane >= to + low - begin) & (lane < to + high - begin), moved, tile)
        tiles.append(tile)
    return jnp.concatenate(tiles, axis=1)


def shifted(table, rows_ref, k):
    for r in range(4):
        rolled = table if r == 0 else pltpu.roll(table, GROUP * r, 1)
        for u in range(5):
            rows_ref[(k * 4 + r) * 5 + u, :TAPS, :] = rolled[:, u * 128 : (u + 1) * 128]


def onward_x(stay, pair):
    return jnp.where(last("gx"), stay, jnp.where(even("gx"), pair[0][T * H :, :], pair[1][T * H :, :]))


def empty_tiles(wa_ref, wb_ref):
    zero = jnp.zeros((T, 128), jnp.bfloat16)
    for q, ref, at in ((0, wa_ref, 3), (1, wb_ref, 0), (2, wb_ref, 1), (3, wa_ref, 0)):
        for part in (0, ref.shape[0] // 2):
            for c in range(TAPS):
                for r in range(4):
                    ref[at + part, pl.ds(place_of(4 * q + r, c), T), :] = zero


def place_of(x, c):
    return (((x // 8) * TAPS + c) * 8 + x % 8) * T


def begin(own_ref, nexty_ref, xa_ref, xb_ref, tables_ref, wa_ref, wb_ref):
    own, nexty = own_ref[T * H :, :], nexty_ref[T * H :, :]
    across = onward_x(own, (xa_ref, xb_ref)) - own
    for k, rows in enumerate((own, 0.25 * across, nexty - own)):
        shifted(expanded(rows), tables_ref, k)
    for r in range(4):
        for u in range(5):
            at = r * 5 + u
            tables_ref[at] = tables_ref[at] + ((r + 0.5) / 4) * tables_ref[at + 20]
    empty_tiles(wa_ref, wb_ref)


def build(own_ref, nexty_ref, arrived, corner, tables_ref, wa_ref, wb_ref, rows_ref, even_ref, odd_ref, use):
    own, nexty = own_ref[T * H :, :], nexty_ref[T * H :, :]
    across = onward_x(own, arrived) - own
    shifted(expanded(0.25 * (onward_x(nexty, corner) - nexty - across)), rows_ref, 1)
    for r in range(4):
        for u in range(5):
            at = r * 5 + u
            rows_ref[at] = tables_ref[at + 40] + ((r + 0.5) / 4) * rows_ref[at + 20]
    along = lax.broadcasted_iota(jnp.int32, (H, Z), 0).astype(jnp.float32)
    steps = [(along + (0.5 + H * half)) / T for half in range(2)]

    def spread(c, q_ref):
        for r in range(4):
            for u in range(5):
                for m in range(2):
                    at = (m * 4 + r) * 5 + u
                    near = tables_ref[at, pl.ds(c, H, stride=0), :]
                    step = rows_ref[at, pl.ds(c, H, stride=0), :]
                    for half in range(2):
                        q_ref[m, r * 5 + u, half * H : (half + 1) * H, :] = pltpu.roll(
                            near + steps[half] * step, H * half, 1, stride=1, stride_axis=0
                        )

    def fill(c, q_ref):
        for r in range(4):
            for u in range(5):
                w, quarter = q_ref[0, r * 5 + u], q_ref[1, r * 5 + u]
                for q in range(4):
                    w = w if q == 0 else w + quarter
                    high = w.astype(jnp.bfloat16)
                    low = (w - high.astype(jnp.float32)).astype(jnp.bfloat16)
                    tile = q + u
                    rows = pl.ds(place_of(4 * q + r, c), T)
                    ref, at, width = (wa_ref, tile - 2, 4) if 2 <= tile < 6 else (wb_ref, tile % 2, 2)
                    ref[at, rows, :] = high
                    ref[at + width, rows, :] = low

    held_refs = (even_ref, odd_ref)
    spread(0, even_ref)
    spread(1, odd_ref)
    fill(0, even_ref)
    for c in range(TAPS):
        use(c)
        if c + 1 < TAPS:
            fill(c + 1, held_refs[(c + 1) % 2])
        if c + 2 < TAPS:
            spread(c + 2, held_refs[c % 2])


def joined(ref, rows):
    return jnp.concatenate([ref[t, rows, :] for t in range(ref.shape[0])], axis=1)


def product(w, v):
    both = jnp.dot(w, v, preferred_element_type=jnp.float32)
    return both[:, :Z] + both[:, Z:]


def inner_part(wide_ref, wa_ref, r_ref):
    v = stationary(wide_ref[...].reshape(T * GROUP, Z))
    for h in range(2):
        rows = slice(h * TAPS * 128, (h + 1) * TAPS * 128)
        r_ref[rows, :] = product(joined(wa_ref, rows), v)


def moved(part, c):
    if c == H:
        return part
    lane = lax.broadcasted_iota(jnp.int32, part.shape, 1)
    return jnp.where((lane >= H - c) & (lane < Z + H - c), pltpu.roll(part, (H - c) % Z, 1), 0.0)


def sides(arrived, corner, side_ref):
    def place(onward, back):
        for h, k in ((0, back), (1, onward)):
            ends = corner[k][: T * H, :].reshape(H, T, Z)
            side_ref[h, :, :H, :] = ends[:, :H]
            side_ref[h, :, H : H + T, :] = arrived[k][: T * H, :].reshape(H, T, Z)
            side_ref[h, :, H + T :, :] = ends[:, H:]

    by_parity("gx", place)


def outer_part(arrived, wb_ref, r_ref, out_ref, side_ref):
    def place(onward, back):
        side_ref[0] = arrived[back][...]
        side_ref[1] = arrived[onward][...]

    by_parity("gx", place)
    for h in range(2):
        v = stationary(side_ref[h].reshape(H * GROUP, Z))
        total = None
        for c in range(TAPS):
            at = slice((h * TAPS + c) * 128, (h * TAPS + c + 1) * 128)
            part = moved(r_ref[at, :] + product(joined(wb_ref, at), v), c)
            total = part if total is None else total + part
        out_ref[h * 8 : (h + 1) * 8] = total.reshape(8, T, Z)


def step_one(d_ref, p_ref, wide_ref, own_ref, nexty_ref, xa_ref, xb_ref, ca_ref, cb_ref, tables_ref, wa_in, wb_in,
             wa_ref, wb_ref, model_ref, first_ref, second_ref, rows_ref,
             even_ref, odd_ref, all_ref, k_ref, side_ref):
    arrived, corner = (xa_ref, xb_ref), (ca_ref, cb_ref)
    sides(arrived, corner, side_ref)
    inner = stationary(wide_ref[...].reshape(T * GROUP, Z))
    for h in range(2):
        all_ref[h, : 4 * 256, :] = inner
        all_ref[h, 4 * 256 :, :] = stationary(side_ref[h].reshape(H * GROUP, Z))

    def use(c):
        for h in range(2):
            at = slice((h * TAPS + c) * 128, (h * TAPS + c + 1) * 128)
            w = jnp.concatenate([joined(wa_ref, at), joined(wb_ref, at)], axis=1)
            part = moved(product(w, all_ref[h]), c)
            k_ref[h] = part if c == 0 else k_ref[h] + part

    build(own_ref, nexty_ref, arrived, corner, tables_ref, wa_ref, wb_ref, rows_ref, even_ref, odd_ref, use)
    v = wide_ref[:, H : H + T, :]
    residual = d_ref[...] - (v + k_ref[...].reshape(T, T, Z))
    model_ref[...] = v + relaxation * p_ref[...] * residual
    columns(model_ref, (first_ref, second_ref))


def step_two(d_ref, p_ref, v_ref, a_ref, b_ref, wb_ref, r_ref, model_ref, residual_ref, k_ref, side_ref):
    outer_part((a_ref, b_ref), wb_ref, r_ref, k_ref, side_ref)
    v = v_ref[...]
    residual = d_ref[...] - (v + k_ref[...])
    residual_ref[...] = residual
    model_ref[...] = v + relaxation * p_ref[...] * residual


def local(data, precond, psf):
    wide_shape = held(T, GROUP, Z)
    block = pltpu.VMEM((T, T, Z), jnp.float32)
    edges = pltpu.VMEM((2, H, GROUP, Z), jnp.float32)
    row, tile = held(T * H + PACKED, Z), held(T, T, Z)
    psf = psf.reshape(DENSE, 1, TAPS)
    v, first, second, xfirst, xsecond, data, precond = call(
        prepare,
        (tile, row, row, row, row, tile, tile),
        4,
        [
            pltpu.VMEM((DENSE + 7, 1, TAPS), jnp.float32),
            pltpu.VMEM((384, 128), jnp.float32),
            pltpu.SemaphoreType.DMA((3,)),
        ],
        pl.BlockSpec(memory_space=pltpu.HBM),
    )(*(pltpu.with_memory_space_constraint(x, pltpu.HBM) for x in (data, precond, psf)))
    a, b = swapped("gy", first, second)
    xa, xb = swapped("gx", xfirst, xsecond)
    wide, cfirst, csecond = call(pack_first, (wide_shape, row, row), 3)(*map(keep, (v, first, a, b)))
    ca, cb = swapped("gx", cfirst, csecond)
    wa, wb = held(8, ROWS, 128, dtype=jnp.bfloat16), held(4, ROWS, 128, dtype=jnp.bfloat16)
    tables, wa_zero, wb_zero = call(begin, (held(60, 24, 128), wa, wb), 2)(*map(keep, (first, cfirst, xa, xb)))
    row = held(T * H, Z)
    turned = pltpu.VMEM((2, 20, T, 128), jnp.float32)
    wa, wb, v, first, second = call(
        step_one,
        (wa, wb, tile, row, row),
        14,
        [
            pltpu.VMEM((40, 24, 128), jnp.float32),
            turned,
            turned,
            pltpu.VMEM((2, 6 * 256, 2 * Z), jnp.bfloat16),
            pltpu.VMEM((2, 128, Z), jnp.float32),
            edges,
        ],
        alias={10: 0, 11: 1},
    )(*map(keep, (data, precond, wide, first, cfirst, xa, xb, ca, cb, tables, wa_zero, wb_zero)))
    a, b = swapped("gy", first, second)
    edge = held(H, GROUP, Z)
    wide, first, second = call(pack_next, (wide_shape, edge, edge), 3)(*map(keep, (v, a, b)))
    a, b = swapped("gx", first, second)
    part = call(inner_part, held(ROWS, Z), 8)(*map(keep, (wide, wa)))
    return call(step_two, (f32(T, T, Z), f32(T, T, Z)), 6, [block, edges])(
        *map(keep, (data, precond, v, a, b, wb, part))
    )


def solution(mesh):
    placed = (P("gx", "gy", None), P("gx", "gy", None), P("gx", "gy", None, None, None))
    return jax.shard_map(
        local,
        mesh=mesh,
        in_specs=placed,
        out_specs=(P("gx", "gy", None), P("gx", "gy", None)),
        check_vma=False,
    )
```

time: 58.8 us -> 60.4 us (1.027)
  starting transfers between devices: 27.2 us -> 33.5 us
  waiting for transfers between devices: 19.2 us -> 13.9 us
    ppermute x8 -> x10, starting transfers between devices: 27.2 us -> 33.5 us  [swapped(): received.append(lax.ppermute(sent, axis, pairs))]
    ppermute x8 -> x10, waiting for transfers between devices: 19.2 us -> 13.9 us  [swapped(): received.append(lax.ppermute(sent, axis, pairs))]
  transfers between devices with their start and end apart: 8 -> 10, of which waited for: 5 -> 4; matrix products, arithmetic and copies ran while one was open for 0% -> 0% of each run, Pallas kernels for 5% -> 6%
where the time goes in v4:
time: 60.4 us; the launch traced here: 59.7 us
  starting transfers between devices  33.5 us (55%)
  waiting for transfers between devices  13.9 us (23%)
  Pallas kernels  11.6 us (19%)
  between operations  0.77 us (1%)
    ppermute x10, starting transfers between devices, swapped(): received.append(lax.ppermute(sent, axis, pairs))  33.5 us
    ppermute x10, waiting for transfers between devices, swapped(): received.append(lax.ppermute(sent, axis, pairs))  13.9 us
    pallas_call x7, Pallas kernels, run(): pl.pallas_call(kernel, out_shape=outs, in_specs=[space] * len(operands),...  11.6 us
  transfers between devices with their start and end apart: 10, of which 4 were waited for; matrix products, arithmetic and copies ran while one was open for 0% of the time, Pallas kernels for 6%

profile of v4, /device:TPU:57, one launch (start us, length us, event | category | flops | bytes accessed | tf_op | source)
XLA Modules:
  0.0 59.7 jit_solution(15575770371866372759)
XLA Ops:
  0.6 1.2 %shard_map.50 = (f32[16,16,128]{2,1,0:T(8,128)S(1)}, f32[168,128]{1,0:T(8,128)S(1)}, f32[168,128]{1,0:T(8,128)S(1)}, f32[168,128]{1,0:T(8,128)S(1)}, f32[168,128...) custom-call(f32[16,16,128]{2,1,0:T(8,128)} %d_hbm.1, f32[16,16,128]{2,1,0:T(8,128)} %p_hbm.1, ...), custom_call_target="tpu_custom_call" | custom-call | tf_op jit(solution)/shard_map/pallas_call | solution.py:34
  1.8 10.3 %collective-permute-start.1 = (f32[168,128]{1,0:T(8,128)S(1)}, f32[168,128]{1,0:T(8,128)S(1)}, u32[]{:S(2)}, u32[]{:S(2)}) collective-permute-start(f32[168,128]{1,0:T(8,128)S(1)} %get-tuple-element.27), channel_id=1, source_target_pairs={{1,2},{2,1},{3,4},{4,3},{5,6},{6,5},{7,8},{8,7},{9,10},{10,9},{11,... | collective-permute-start | bytes 258056 | tf_op jit(solution)/shard_map/ppermute | solution.py:62
  12.1 0.1 collective-permute-start
  12.2 1.0 %collective-permute-start.2 = (f32[168,128]{1,0:T(8,128)S(1)}, f32[168,128]{1,0:T(8,128)S(1)}, u32[]{:S(2)}, u32[]{:S(2)}) collective-permute-start(f32[168,128]{1,0:T(8,128)S(1)} %get-tuple-element.30), channel_id=1, source_target_pairs={{0,32},{32,0},{64,96},{96,64},{128,160},{160,128},{192,224},{224,1... | collective-permute-start | bytes 258056 | tf_op jit(solution)/shard_map/ppermute | solution.py:62
  13.3 2.5 %collective-permute-start.3 = (f32[168,128]{1,0:T(8,128)S(1)}, f32[168,128]{1,0:T(8,128)S(1)}, u32[]{:S(2)}, u32[]{:S(2)}) collective-permute-start(f32[168,128]{1,0:T(8,128)S(1)} %get-tuple-element.31), channel_id=1, source_target_pairs={{32,64},{64,32},{96,128},{128,96},{160,192},{192,160},{33,65},{65,... | collective-permute-start | bytes 258056 | tf_op jit(solution)/shard_map/ppermute | solution.py:62
  15.8 0.0 collective-permute-done.1.b_ref
  15.8 3.7 %collective-permute-done.a_ref = f32[168,128]{1,0:T(8,128)S(1)} collective-permute-done((f32[168,128]{1,0:T(8,128)S(1)}, f32[168,128]{1,0:T(8,128)S(1)}, u32[]{:S(2)}, u32[]{:S(2)}) %collective-permute-start) | collective-permute-done | bytes 86048 | tf_op jit(solution)/shard_map/ppermute | solution.py:62
  19.5 0.1 shard_map.51
  19.6 6.6 %collective-permute-start.5 = (f32[168,128]{1,0:T(8,128)S(1)}, f32[168,128]{1,0:T(8,128)S(1)}, u32[]{:S(2)}, u32[]{:S(2)}) collective-permute-start(f32[168,128]{1,0:T(8,128)S(1)} %get-tuple-element.32), channel_id=1, source_target_pairs={{32,64},{64,32},{96,128},{128,96},{160,192},{192,160},{33,65},{65,... | collective-permute-start | bytes 258056 | tf_op jit(solution)/shard_map/ppermute | solution.py:62
  26.2 0.1 collective-permute-start.4
  26.3 0.0 collective-permute-done.2.xa_ref
  26.3 0.8 %shard_map.52 = (f32[60,24,128]{2,1,0:T(8,128)S(1)}, bf16[8,4352,128]{2,1,0:T(8,128)(2,1)S(1)}, bf16[4,4352,128]{2,1,0:T(8,128)(2,1)S(1)}) custom-call(f32[168,128]{1,0:T(8,128)S(1)} %get-tuple-element.26.own_ref, f32[168,128]{1,0:T(8,128)S(1)} %get-tuple-element.29.nexty_ref, f32[168,128]{1,0:T(8,128)S(1)} %collective-permute-done.2.xa_ref, ...), custom_call_target="tpu_custom_call" | custom-call | tf_op jit(solution)/shard_map/pallas_call | solution.py:34
  27.1 1.2 %collective-permute-done.5.cb_ref = f32[168,128]{1,0:T(8,128)S(1)} collective-permute-done((f32[168,128]{1,0:T(8,128)S(1)}, f32[168,128]{1,0:T(8,128)S(1)}, u32[]{:S(2)}, u32[]{:S(2)}) %collective-permute-start.5) | collective-permute-done | bytes 86048 | tf_op jit(solution)/shard_map/ppermute | solution.py:62
  28.4 4.8 %shard_map.53 = (bf16[8,4352,128]{2,1,0:T(8,128)(2,1)S(1)}, bf16[4,4352,128]{2,1,0:T(8,128)(2,1)S(1)}, f32[16,16,128]{2,1,0:T(8,128)S(1)}, f32[128,128]{1,0:T(8,128)S(1)}, f32[128,128]{1,0:T(8,128)S(1)}) custom-call(f32[16,16,128]{2,1,0:T(8,128)S(1)} %get-tuple-element.23.d_ref, ...), custom_call_target="tpu_custom_call", output_to_operand_aliasing={{0}: (10, {}), {1}: (11, {})} | custom-call | tf_op jit(solution)/shard_map/pallas_call | solution.py:34
  33.1 3.9 %collective-permute-start.6 = (f32[128,128]{1,0:T(8,128)S(1)}, f32[128,128]{1,0:T(8,128)S(1)}, u32[]{:S(2)}, u32[]{:S(2)}) collective-permute-start(f32[128,128]{1,0:T(8,128)S(1)} %get-tuple-element.37), channel_id=1, source_target_pairs={{0,1},{1,0},{2,3},{3,2},{4,5},{5,4},{6,7},{7,6},{8,9},{9,8},{10,11... | collective-permute-start | bytes 196616 | tf_op jit(solution)/shard_map/ppermute | solution.py:62
  37.0 3.3 %collective-permute-start.7 = (f32[128,128]{1,0:T(8,128)S(1)}, f32[128,128]{1,0:T(8,128)S(1)}, u32[]{:S(2)}, u32[]{:S(2)}) collective-permute-start(f32[128,128]{1,0:T(8,128)S(1)} %get-tuple-element.38), channel_id=1, source_target_pairs={{1,2},{2,1},{3,4},{4,3},{5,6},{6,5},{7,8},{8,7},{9,10},{10,9},{11,... | collective-permute-start | bytes 196616 | tf_op jit(solution)/shard_map/ppermute | solution.py:62
  40.3 1.9 %collective-permute-done.6.a_ref = f32[128,128]{1,0:T(8,128)S(1)} collective-permute-done((f32[128,128]{1,0:T(8,128)S(1)}, f32[128,128]{1,0:T(8,128)S(1)}, u32[]{:S(2)}, u32[]{:S(2)}) %collective-permute-start.6) | collective-permute-done | bytes 65568 | tf_op jit(solution)/shard_map/ppermute | solution.py:62
  42.1 7.0 %collective-permute-done.7.b_ref = f32[128,128]{1,0:T(8,128)S(1)} collective-permute-done((f32[128,128]{1,0:T(8,128)S(1)}, f32[128,128]{1,0:T(8,128)S(1)}, u32[]{:S(2)}, u32[]{:S(2)}) %collective-permute-start.7) | collective-permute-done | bytes 65568 | tf_op jit(solution)/shard_map/ppermute | solution.py:62
  49.1 0.1 shard_map.54
  49.2 1.6 %collective-permute-start.8 = (f32[8,32,128]{2,1,0:T(8,128)S(1)}, f32[8,32,128]{2,1,0:T(8,128)S(1)}, u32[]{:S(2)}, u32[]{:S(2)}) collective-permute-start(f32[8,32,128]{2,1,0:T(8,128)S(1)} %get-tuple-element.39), channel_id=1, source_target_pairs={{0,32},{32,0},{64,96},{96,64},{128,160},{160,128},{192,224},{224,1... | collective-permute-start | bytes 393224 | tf_op jit(solution)/shard_map/ppermute | solution.py:62
  50.8 4.1 %collective-permute-start.9 = (f32[8,32,128]{2,1,0:T(8,128)S(1)}, f32[8,32,128]{2,1,0:T(8,128)S(1)}, u32[]{:S(2)}, u32[]{:S(2)}) collective-permute-start(f32[8,32,128]{2,1,0:T(8,128)S(1)} %get-tuple-element.40), channel_id=1, source_target_pairs={{32,64},{64,32},{96,128},{128,96},{160,192},{192,160},{33,65},{65,... | collective-permute-start | bytes 393224 | tf_op jit(solution)/shard_map/ppermute | solution.py:62
  54.9 2.6 %shard_map.55.r_ref = f32[4352,128]{1,0:T(8,128)S(1)} custom-call(f32[16,32,128]{2,1,0:T(8,128)S(1)} %get-tuple-element.42.wide_ref, bf16[8,4352,128]{2,1,0:T(8,128)(2,1)S(1)} %get-tuple-element.43.wa_ref), custom_call_target="tpu_custom_call" | custom-call | tf_op jit(solution)/shard_map/pallas_call | solution.py:34
  57.5 0.0 collective-permute-done.9.b_ref
  57.6 2.1 %shard_map.56 = (f32[16,16,128]{2,1,0:T(8,128)}, f32[16,16,128]{2,1,0:T(8,128)}) custom-call(f32[16,16,128]{2,1,0:T(8,128)S(1)} %get-tuple-element.23.d_ref, f32[16,16,128]{2,1,0:T(8,128)S(1)} %get-tuple-element.24.p_ref, f32[16,16,128]{2,1,0:T(8,128)S(1)} %get-tuple-element.36.v_ref, f32[8,32,128]{2,1,0:T(8,128)S(1)} %collective-permute-done.8.a_ref, ...), custom_call_target="tpu_custom_call" | custom-call | tf_op jit(solution)/shard_map/pallas_call | solution.py:34
  (3 shorter events, 0.0 us)
Async XLA Ops:
  1.8 14.0 %collective-permute-start.1 = (f32[168,128]{1,0:T(8,128)S(1)}, f32[168,128]{1,0:T(8,128)S(1)}, u32[]{:S(2)}, u32[]{:S(2)}) collective-permute-start(f32[168,128]{1,0:T(8,128)S(1)} %get-tuple-element.27), channel_id=1, source_target_pairs={{1,2},{2,1},{3,4},{4,3},{5,6},{6,5},{7,8},{8,7},{9,10},{10,9},{11,... | collective-permute-start | bytes 258056 | tf_op jit(solution)/shard_map/ppermute | solution.py:62
  12.1 7.4 %collective-permute-start = (f32[168,128]{1,0:T(8,128)S(1)}, f32[168,128]{1,0:T(8,128)S(1)}, u32[]{:S(2)}, u32[]{:S(2)}) collective-permute-start(f32[168,128]{1,0:T(8,128)S(1)} %get-tuple-element.26.own_ref), channel_id=1, source_target_pairs={{0,1},{1,0},{2,3},{3,2},{4,5},{5,4},{6,7},{7,6},{8,9},{9,8},{10,11... | collective-permute-start | bytes 258056 | tf_op jit(solution)/shard_map/ppermute | solution.py:62
  12.2 14.1 %collective-permute-start.2 = (f32[168,128]{1,0:T(8,128)S(1)}, f32[168,128]{1,0:T(8,128)S(1)}, u32[]{:S(2)}, u32[]{:S(2)}) collective-permute-start(f32[168,128]{1,0:T(8,128)S(1)} %get-tuple-element.30), channel_id=1, source_target_pairs={{0,32},{32,0},{64,96},{96,64},{128,160},{160,128},{192,224},{224,1... | collective-permute-start | bytes 258056 | tf_op jit(solution)/shard_map/ppermute | solution.py:62
  13.3 13.1 %collective-permute-start.3 = (f32[168,128]{1,0:T(8,128)S(1)}, f32[168,128]{1,0:T(8,128)S(1)}, u32[]{:S(2)}, u32[]{:S(2)}) collective-permute-start(f32[168,128]{1,0:T(8,128)S(1)} %get-tuple-element.31), channel_id=1, source_target_pairs={{32,64},{64,32},{96,128},{128,96},{160,192},{192,160},{33,65},{65,... | collective-permute-start | bytes 258056 | tf_op jit(solution)/shard_map/ppermute | solution.py:62
  19.6 8.8 %collective-permute-start.5 = (f32[168,128]{1,0:T(8,128)S(1)}, f32[168,128]{1,0:T(8,128)S(1)}, u32[]{:S(2)}, u32[]{:S(2)}) collective-permute-start(f32[168,128]{1,0:T(8,128)S(1)} %get-tuple-element.32), channel_id=1, source_target_pairs={{32,64},{64,32},{96,128},{128,96},{160,192},{192,160},{33,65},{65,... | collective-permute-start | bytes 258056 | tf_op jit(solution)/shard_map/ppermute | solution.py:62
  26.2 2.2 %collective-permute-start.4 = (f32[168,128]{1,0:T(8,128)S(1)}, f32[168,128]{1,0:T(8,128)S(1)}, u32[]{:S(2)}, u32[]{:S(2)}) collective-permute-start(f32[168,128]{1,0:T(8,128)S(1)} %get-tuple-element.29.nexty_ref), channel_id=1, source_target_pairs={{0,32},{32,0},{64,96},{96,64},{128,160},{160,128},{192,224},{224,1... | collective-permute-start | bytes 258056 | tf_op jit(solution)/shard_map/ppermute | solution.py:62
  33.1 9.0 %collective-permute-start.6 = (f32[128,128]{1,0:T(8,128)S(1)}, f32[128,128]{1,0:T(8,128)S(1)}, u32[]{:S(2)}, u32[]{:S(2)}) collective-permute-start(f32[128,128]{1,0:T(8,128)S(1)} %get-tuple-element.37), channel_id=1, source_target_pairs={{0,1},{1,0},{2,3},{3,2},{4,5},{5,4},{6,7},{7,6},{8,9},{9,8},{10,11... | collective-permute-start | bytes 196616 | tf_op jit(solution)/shard_map/ppermute | solution.py:62
  37.0 12.1 %collective-permute-start.7 = (f32[128,128]{1,0:T(8,128)S(1)}, f32[128,128]{1,0:T(8,128)S(1)}, u32[]{:S(2)}, u32[]{:S(2)}) collective-permute-start(f32[128,128]{1,0:T(8,128)S(1)} %get-tuple-element.38), channel_id=1, source_target_pairs={{1,2},{2,1},{3,4},{4,3},{5,6},{6,5},{7,8},{8,7},{9,10},{10,9},{11,... | collective-permute-start | bytes 196616 | tf_op jit(solution)/shard_map/ppermute | solution.py:62
  49.2 8.3 %collective-permute-start.8 = (f32[8,32,128]{2,1,0:T(8,128)S(1)}, f32[8,32,128]{2,1,0:T(8,128)S(1)}, u32[]{:S(2)}, u32[]{:S(2)}) collective-permute-start(f32[8,32,128]{2,1,0:T(8,128)S(1)} %get-tuple-element.39), channel_id=1, source_target_pairs={{0,32},{32,0},{64,96},{96,64},{128,160},{160,128},{192,224},{224,1... | collective-permute-start | bytes 393224 | tf_op jit(solution)/shard_map/ppermute | solution.py:62
  50.8 6.8 %collective-permute-start.9 = (f32[8,32,128]{2,1,0:T(8,128)S(1)}, f32[8,32,128]{2,1,0:T(8,128)S(1)}, u32[]{:S(2)}, u32[]{:S(2)}) collective-permute-start(f32[8,32,128]{2,1,0:T(8,128)S(1)} %get-tuple-element.40), channel_id=1, source_target_pairs={{32,64},{64,32},{96,128},{128,96},{160,192},{192,160},{33,65},{65,... | collective-permute-start | bytes 393224 | tf_op jit(solution)/shard_map/ppermute | solution.py:62

commit v5 on v4

--- a/solution.py
+++ b/solution.py
@@ -326,19 +326,18 @@
 
 def step_one(d_ref, p_ref, wide_ref, own_ref, nexty_ref, xa_ref, xb_ref, ca_ref, cb_ref, tables_ref, wa_in, wb_in,
              wa_ref, wb_ref, model_ref, first_ref, second_ref, rows_ref,
-             even_ref, odd_ref, all_ref, k_ref, side_ref):
+             even_ref, odd_ref, inner_ref, outer_ref, k_ref, side_ref):
     arrived, corner = (xa_ref, xb_ref), (ca_ref, cb_ref)
     sides(arrived, corner, side_ref)
-    inner = stationary(wide_ref[...].reshape(T * GROUP, Z))
+    inner_ref[...] = halves(wide_ref[...].reshape(T * GROUP, Z))
     for h in range(2):
-        all_ref[h, : 4 * 256, :] = inner
-        all_ref[h, 4 * 256 :, :] = stationary(side_ref[h].reshape(H * GROUP, Z))
+        outer_ref[h] = halves(side_ref[h].reshape(H * GROUP, Z))
 
     def use(c):
         for h in range(2):
             at = slice((h * TAPS + c) * 128, (h * TAPS + c + 1) * 128)
             w = jnp.concatenate([joined(wa_ref, at), joined(wb_ref, at)], axis=1)
-            part = moved(product(w, all_ref[h]), c)
+            part = moved(product(w, jnp.concatenate([inner_ref[...]] * 2 + [outer_ref[h]] * 2, axis=0)), c)
             k_ref[h] = part if c == 0 else k_ref[h] + part
 
     build(own_ref, nexty_ref, arrived, corner, tables_ref, wa_ref, wb_ref, rows_ref, even_ref, odd_ref, use)
@@ -389,7 +388,8 @@
             pltpu.VMEM((40, 24, 128), jnp.float32),
             turned,
             turned,
-            pltpu.VMEM((2, 6 * 256, 2 * Z), jnp.bfloat16),
+            pltpu.VMEM((T * GROUP, 2 * Z), jnp.bfloat16),
+            pltpu.VMEM((2, H * GROUP, 2 * Z), jnp.bfloat16),
             pltpu.VMEM((2, 128, Z), jnp.float32),
             edges,
         ],

time: 60.4 us -> 60.4 us (level)
  no operation moved by 1% of the time
where the time goes in v5:
time: 60.4 us; the launch traced here: 59.7 us
  starting transfers between devices  33.5 us (55%)
  waiting for transfers between devices  13.9 us (23%)
  Pallas kernels  11.6 us (19%)
  between operations  0.77 us (1%)
    ppermute x10, starting transfers between devices, swapped(): received.append(lax.ppermute(sent, axis, pairs))  33.5 us
    ppermute x10, waiting for transfers between devices, swapped(): received.append(lax.ppermute(sent, axis, pairs))  13.9 us
    pallas_call x7, Pallas kernels, run(): pl.pallas_call(kernel, out_shape=outs, in_specs=[space] * len(operands),...  11.6 us
  transfers between devices with their start and end apart: 10, of which 4 were waited for; matrix products, arithmetic and copies ran while one was open for 0% of the time, Pallas kernels for 6%

profile of v5, /device:TPU:57, one launch (start us, length us, event | category | flops | bytes accessed | tf_op | source)
XLA Modules:
  0.0 59.7 jit_solution(15575770371866372759)
XLA Ops:
  0.6 1.2 %shard_map.50 = (f32[16,16,128]{2,1,0:T(8,128)S(1)}, f32[168,128]{1,0:T(8,128)S(1)}, f32[168,128]{1,0:T(8,128)S(1)}, f32[168,128]{1,0:T(8,128)S(1)}, f32[168,128...) custom-call(f32[16,16,128]{2,1,0:T(8,128)} %d_hbm.1, f32[16,16,128]{2,1,0:T(8,128)} %p_hbm.1, ...), custom_call_target="tpu_custom_call" | custom-call | tf_op jit(solution)/shard_map/pallas_call | solution.py:34
  1.8 10.3 %collective-permute-start.1 = (f32[168,128]{1,0:T(8,128)S(1)}, f32[168,128]{1,0:T(8,128)S(1)}, u32[]{:S(2)}, u32[]{:S(2)}) collective-permute-start(f32[168,128]{1,0:T(8,128)S(1)} %get-tuple-element.27), channel_id=1, source_target_pairs={{1,2},{2,1},{3,4},{4,3},{5,6},{6,5},{7,8},{8,7},{9,10},{10,9},{11,... | collective-permute-start | bytes 258056 | tf_op jit(solution)/shard_map/ppermute | solution.py:62
  12.1 0.1 collective-permute-start
  12.2 1.0 %collective-permute-start.2 = (f32[168,128]{1,0:T(8,128)S(1)}, f32[168,128]{1,0:T(8,128)S(1)}, u32[]{:S(2)}, u32[]{:S(2)}) collective-permute-start(f32[168,128]{1,0:T(8,128)S(1)} %get-tuple-element.30), channel_id=1, source_target_pairs={{0,32},{32,0},{64,96},{96,64},{128,160},{160,128},{192,224},{224,1... | collective-permute-start | bytes 258056 | tf_op jit(solution)/shard_map/ppermute | solution.py:62
  13.3 2.5 %collective-permute-start.3 = (f32[168,128]{1,0:T(8,128)S(1)}, f32[168,128]{1,0:T(8,128)S(1)}, u32[]{:S(2)}, u32[]{:S(2)}) collective-permute-start(f32[168,128]{1,0:T(8,128)S(1)} %get-tuple-element.31), channel_id=1, source_target_pairs={{32,64},{64,32},{96,128},{128,96},{160,192},{192,160},{33,65},{65,... | collective-permute-start | bytes 258056 | tf_op jit(solution)/shard_map/ppermute | solution.py:62
  15.8 0.0 collective-permute-done.1.b_ref
  15.8 3.7 %collective-permute-done.a_ref = f32[168,128]{1,0:T(8,128)S(1)} collective-permute-done((f32[168,128]{1,0:T(8,128)S(1)}, f32[168,128]{1,0:T(8,128)S(1)}, u32[]{:S(2)}, u32[]{:S(2)}) %collective-permute-start) | collective-permute-done | bytes 86048 | tf_op jit(solution)/shard_map/ppermute | solution.py:62
  19.5 0.1 shard_map.51
  19.6 6.6 %collective-permute-start.5 = (f32[168,128]{1,0:T(8,128)S(1)}, f32[168,128]{1,0:T(8,128)S(1)}, u32[]{:S(2)}, u32[]{:S(2)}) collective-permute-start(f32[168,128]{1,0:T(8,128)S(1)} %get-tuple-element.32), channel_id=1, source_target_pairs={{32,64},{64,32},{96,128},{128,96},{160,192},{192,160},{33,65},{65,... | collective-permute-start | bytes 258056 | tf_op jit(solution)/shard_map/ppermute | solution.py:62
  26.2 0.1 collective-permute-start.4
  26.3 0.0 collective-permute-done.2.xa_ref
  26.3 0.8 %shard_map.52 = (f32[60,24,128]{2,1,0:T(8,128)S(1)}, bf16[8,4352,128]{2,1,0:T(8,128)(2,1)S(1)}, bf16[4,4352,128]{2,1,0:T(8,128)(2,1)S(1)}) custom-call(f32[168,128]{1,0:T(8,128)S(1)} %get-tuple-element.26.own_ref, f32[168,128]{1,0:T(8,128)S(1)} %get-tuple-element.29.nexty_ref, f32[168,128]{1,0:T(8,128)S(1)} %collective-permute-done.2.xa_ref, ...), custom_call_target="tpu_custom_call" | custom-call | tf_op jit(solution)/shard_map/pallas_call | solution.py:34
  27.1 1.2 %collective-permute-done.5.cb_ref = f32[168,128]{1,0:T(8,128)S(1)} collective-permute-done((f32[168,128]{1,0:T(8,128)S(1)}, f32[168,128]{1,0:T(8,128)S(1)}, u32[]{:S(2)}, u32[]{:S(2)}) %collective-permute-start.5) | collective-permute-done | bytes 86048 | tf_op jit(solution)/shard_map/ppermute | solution.py:62
  28.4 4.8 %shard_map.53 = (bf16[8,4352,128]{2,1,0:T(8,128)(2,1)S(1)}, bf16[4,4352,128]{2,1,0:T(8,128)(2,1)S(1)}, f32[16,16,128]{2,1,0:T(8,128)S(1)}, f32[128,128]{1,0:T(8,128)S(1)}, f32[128,128]{1,0:T(8,128)S(1)}) custom-call(f32[16,16,128]{2,1,0:T(8,128)S(1)} %get-tuple-element.23.d_ref, ...), custom_call_target="tpu_custom_call", output_to_operand_aliasing={{0}: (10, {}), {1}: (11, {})} | custom-call | tf_op jit(solution)/shard_map/pallas_call | solution.py:34
  33.1 3.9 %collective-permute-start.6 = (f32[128,128]{1,0:T(8,128)S(1)}, f32[128,128]{1,0:T(8,128)S(1)}, u32[]{:S(2)}, u32[]{:S(2)}) collective-permute-start(f32[128,128]{1,0:T(8,128)S(1)} %get-tuple-element.37), channel_id=1, source_target_pairs={{0,1},{1,0},{2,3},{3,2},{4,5},{5,4},{6,7},{7,6},{8,9},{9,8},{10,11... | collective-permute-start | bytes 196616 | tf_op jit(solution)/shard_map/ppermute | solution.py:62
  37.0 3.3 %collective-permute-start.7 = (f32[128,128]{1,0:T(8,128)S(1)}, f32[128,128]{1,0:T(8,128)S(1)}, u32[]{:S(2)}, u32[]{:S(2)}) collective-permute-start(f32[128,128]{1,0:T(8,128)S(1)} %get-tuple-element.38), channel_id=1, source_target_pairs={{1,2},{2,1},{3,4},{4,3},{5,6},{6,5},{7,8},{8,7},{9,10},{10,9},{11,... | collective-permute-start | bytes 196616 | tf_op jit(solution)/shard_map/ppermute | solution.py:62
  40.3 1.9 %collective-permute-done.6.a_ref = f32[128,128]{1,0:T(8,128)S(1)} collective-permute-done((f32[128,128]{1,0:T(8,128)S(1)}, f32[128,128]{1,0:T(8,128)S(1)}, u32[]{:S(2)}, u32[]{:S(2)}) %collective-permute-start.6) | collective-permute-done | bytes 65568 | tf_op jit(solution)/shard_map/ppermute | solution.py:62
  42.1 7.0 %collective-permute-done.7.b_ref = f32[128,128]{1,0:T(8,128)S(1)} collective-permute-done((f32[128,128]{1,0:T(8,128)S(1)}, f32[128,128]{1,0:T(8,128)S(1)}, u32[]{:S(2)}, u32[]{:S(2)}) %collective-permute-start.7) | collective-permute-done | bytes 65568 | tf_op jit(solution)/shard_map/ppermute | solution.py:62
  49.1 0.1 shard_map.54
  49.2 1.6 %collective-permute-start.8 = (f32[8,32,128]{2,1,0:T(8,128)S(1)}, f32[8,32,128]{2,1,0:T(8,128)S(1)}, u32[]{:S(2)}, u32[]{:S(2)}) collective-permute-start(f32[8,32,128]{2,1,0:T(8,128)S(1)} %get-tuple-element.39), channel_id=1, source_target_pairs={{0,32},{32,0},{64,96},{96,64},{128,160},{160,128},{192,224},{224,1... | collective-permute-start | bytes 393224 | tf_op jit(solution)/shard_map/ppermute | solution.py:62
  50.8 4.1 %collective-permute-start.9 = (f32[8,32,128]{2,1,0:T(8,128)S(1)}, f32[8,32,128]{2,1,0:T(8,128)S(1)}, u32[]{:S(2)}, u32[]{:S(2)}) collective-permute-start(f32[8,32,128]{2,1,0:T(8,128)S(1)} %get-tuple-element.40), channel_id=1, source_target_pairs={{32,64},{64,32},{96,128},{128,96},{160,192},{192,160},{33,65},{65,... | collective-permute-start | bytes 393224 | tf_op jit(solution)/shard_map/ppermute | solution.py:62
  54.9 2.6 %shard_map.55.r_ref = f32[4352,128]{1,0:T(8,128)S(1)} custom-call(f32[16,32,128]{2,1,0:T(8,128)S(1)} %get-tuple-element.42.wide_ref, bf16[8,4352,128]{2,1,0:T(8,128)(2,1)S(1)} %get-tuple-element.43.wa_ref), custom_call_target="tpu_custom_call" | custom-call | tf_op jit(solution)/shard_map/pallas_call | solution.py:34
  57.5 0.0 collective-permute-done.9.b_ref
  57.6 2.1 %shard_map.56 = (f32[16,16,128]{2,1,0:T(8,128)}, f32[16,16,128]{2,1,0:T(8,128)}) custom-call(f32[16,16,128]{2,1,0:T(8,128)S(1)} %get-tuple-element.23.d_ref, f32[16,16,128]{2,1,0:T(8,128)S(1)} %get-tuple-element.24.p_ref, f32[16,16,128]{2,1,0:T(8,128)S(1)} %get-tuple-element.36.v_ref, f32[8,32,128]{2,1,0:T(8,128)S(1)} %collective-permute-done.8.a_ref, ...), custom_call_target="tpu_custom_call" | custom-call | tf_op jit(solution)/shard_map/pallas_call | solution.py:34
  (3 shorter events, 0.0 us)
Async XLA Ops:
  1.8 14.0 %collective-permute-start.1 = (f32[168,128]{1,0:T(8,128)S(1)}, f32[168,128]{1,0:T(8,128)S(1)}, u32[]{:S(2)}, u32[]{:S(2)}) collective-permute-start(f32[168,128]{1,0:T(8,128)S(1)} %get-tuple-element.27), channel_id=1, source_target_pairs={{1,2},{2,1},{3,4},{4,3},{5,6},{6,5},{7,8},{8,7},{9,10},{10,9},{11,... | collective-permute-start | bytes 258056 | tf_op jit(solution)/shard_map/ppermute | solution.py:62
  12.1 7.4 %collective-permute-start = (f32[168,128]{1,0:T(8,128)S(1)}, f32[168,128]{1,0:T(8,128)S(1)}, u32[]{:S(2)}, u32[]{:S(2)}) collective-permute-start(f32[168,128]{1,0:T(8,128)S(1)} %get-tuple-element.26.own_ref), channel_id=1, source_target_pairs={{0,1},{1,0},{2,3},{3,2},{4,5},{5,4},{6,7},{7,6},{8,9},{9,8},{10,11... | collective-permute-start | bytes 258056 | tf_op jit(solution)/shard_map/ppermute | solution.py:62
  12.2 14.1 %collective-permute-start.2 = (f32[168,128]{1,0:T(8,128)S(1)}, f32[168,128]{1,0:T(8,128)S(1)}, u32[]{:S(2)}, u32[]{:S(2)}) collective-permute-start(f32[168,128]{1,0:T(8,128)S(1)} %get-tuple-element.30), channel_id=1, source_target_pairs={{0,32},{32,0},{64,96},{96,64},{128,160},{160,128},{192,224},{224,1... | collective-permute-start | bytes 258056 | tf_op jit(solution)/shard_map/ppermute | solution.py:62
  13.3 13.1 %collective-permute-start.3 = (f32[168,128]{1,0:T(8,128)S(1)}, f32[168,128]{1,0:T(8,128)S(1)}, u32[]{:S(2)}, u32[]{:S(2)}) collective-permute-start(f32[168,128]{1,0:T(8,128)S(1)} %get-tuple-element.31), channel_id=1, source_target_pairs={{32,64},{64,32},{96,128},{128,96},{160,192},{192,160},{33,65},{65,... | collective-permute-start | bytes 258056 | tf_op jit(solution)/shard_map/ppermute | solution.py:62
  19.6 8.8 %collective-permute-start.5 = (f32[168,128]{1,0:T(8,128)S(1)}, f32[168,128]{1,0:T(8,128)S(1)}, u32[]{:S(2)}, u32[]{:S(2)}) collective-permute-start(f32[168,128]{1,0:T(8,128)S(1)} %get-tuple-element.32), channel_id=1, source_target_pairs={{32,64},{64,32},{96,128},{128,96},{160,192},{192,160},{33,65},{65,... | collective-permute-start | bytes 258056 | tf_op jit(solution)/shard_map/ppermute | solution.py:62
  26.2 2.2 %collective-permute-start.4 = (f32[168,128]{1,0:T(8,128)S(1)}, f32[168,128]{1,0:T(8,128)S(1)}, u32[]{:S(2)}, u32[]{:S(2)}) collective-permute-start(f32[168,128]{1,0:T(8,128)S(1)} %get-tuple-element.29.nexty_ref), channel_id=1, source_target_pairs={{0,32},{32,0},{64,96},{96,64},{128,160},{160,128},{192,224},{224,1... | collective-permute-start | bytes 258056 | tf_op jit(solution)/shard_map/ppermute | solution.py:62
  33.1 9.0 %collective-permute-start.6 = (f32[128,128]{1,0:T(8,128)S(1)}, f32[128,128]{1,0:T(8,128)S(1)}, u32[]{:S(2)}, u32[]{:S(2)}) collective-permute-start(f32[128,128]{1,0:T(8,128)S(1)} %get-tuple-element.37), channel_id=1, source_target_pairs={{0,1},{1,0},{2,3},{3,2},{4,5},{5,4},{6,7},{7,6},{8,9},{9,8},{10,11... | collective-permute-start | bytes 196616 | tf_op jit(solution)/shard_map/ppermute | solution.py:62
  37.0 12.1 %collective-permute-start.7 = (f32[128,128]{1,0:T(8,128)S(1)}, f32[128,128]{1,0:T(8,128)S(1)}, u32[]{:S(2)}, u32[]{:S(2)}) collective-permute-start(f32[128,128]{1,0:T(8,128)S(1)} %get-tuple-element.38), channel_id=1, source_target_pairs={{1,2},{2,1},{3,4},{4,3},{5,6},{6,5},{7,8},{8,7},{9,10},{10,9},{11,... | collective-permute-start | bytes 196616 | tf_op jit(solution)/shard_map/ppermute | solution.py:62
  49.2 8.3 %collective-permute-start.8 = (f32[8,32,128]{2,1,0:T(8,128)S(1)}, f32[8,32,128]{2,1,0:T(8,128)S(1)}, u32[]{:S(2)}, u32[]{:S(2)}) collective-permute-start(f32[8,32,128]{2,1,0:T(8,128)S(1)} %get-tuple-element.39), channel_id=1, source_target_pairs={{0,32},{32,0},{64,96},{96,64},{128,160},{160,128},{192,224},{224,1... | collective-permute-start | bytes 393224 | tf_op jit(solution)/shard_map/ppermute | solution.py:62
  50.8 6.8 %collective-permute-start.9 = (f32[8,32,128]{2,1,0:T(8,128)S(1)}, f32[8,32,128]{2,1,0:T(8,128)S(1)}, u32[]{:S(2)}, u32[]{:S(2)}) collective-permute-start(f32[8,32,128]{2,1,0:T(8,128)S(1)} %get-tuple-element.40), channel_id=1, source_target_pairs={{32,64},{64,32},{96,128},{128,96},{160,192},{192,160},{33,65},{65,... | collective-permute-start | bytes 393224 | tf_op jit(solution)/shard_map/ppermute | solution.py:62
